TPU v7x, 32 devices: a whole 2x2x4 slice. The times are simulated.
32 devices in a mesh: pix: 8 (over z, y), lat: 4 (over x, core).
Axes of the slice: x: 2, y: 2, z: 4, core: 2. Of those that a mesh axis runs over, the one named last changes fastest.
Arguments:
- latents: float32 [2048, 512], P('lat'), as said below
- pixel_keys: float32 [4096, 512], P('pix'), as said below
- pixel_values: float32 [4096, 512], P('pix'), may hold values from -6 to 6
- norm_gain: float32 [512], replicated, may hold values from 0.1 to 1.9
- w_key: float32 [512, 512], replicated, may hold values from -0.25 to 0.25
- w_value: float32 [512, 512], replicated, may hold values from -0.25 to 0.25
- pixel_queries: float32 [4096, 512], P('pix'), as said below
Outputs:
- latent_state: float32 [2048, 512], P('lat')
- pixel_out: float32 [4096, 512], P('pix')
Inputs may be any that keep to these rules, and one draw needn't show every extreme that they name: Real-valued latents. `pixel_keys`: Real-valued keys. `pixel_queries`: Real-valued queries.
All inputs are finite; a program needn't handle non-finite values.
Results may differ from a plain program's by a relative error of at most 0.0003.
Values sent between devices are 32-bit elements; how exact they have to be, the bound alone decides.
No kernel may reach another device: no remote copies, remote signals or barrier semaphores. Data moves between devices by JAX's collectives and lax.ppermute only.
A program may use at most 64 MiB of HBM per device.

v0:
```python
import jax
import jax.numpy as jnp
from jax import lax
from jax.sharding import PartitionSpec as P


def joined(value, axis, join):
    pieces = jax.tree.map(lambda part: lax.all_gather(part, axis), value)
    head = jax.tree.map(lambda part: part[0], pieces)
    tail = jax.tree.map(lambda part: part[1:], pieces)
    running, _ = lax.scan(lambda running, slab: (join(running, slab), None), head, tail)
    return running


def partials(queries, keys, values):
    scores = jnp.dot(queries, keys.T, precision=lax.Precision.HIGHEST) / jnp.sqrt(
        jnp.float32(keys.shape[1])
    )
    top = jnp.max(scores, axis=1)
    weights = jnp.exp(scores - top[:, None])
    total = jnp.sum(weights, axis=1)
    weighted = jnp.dot(weights, values, precision=lax.Precision.HIGHEST)
    return (top, total, weighted)


def combine_parts(first, second):
    top = jnp.maximum(first[0], second[0])
    scale_a = jnp.exp(first[0] - top)
    scale_b = jnp.exp(second[0] - top)
    total = first[1] * scale_a + second[1] * scale_b
    weighted = first[2] * scale_a[:, None] + second[2] * scale_b[:, None]
    return (top, total, weighted)


def project(state, norm_gain, w_key, w_value):
    normed = state / jnp.sqrt(jnp.mean(state * state, axis=1, keepdims=True) + 1e-06) * norm_gain
    keys_new = jnp.dot(normed, w_key, precision=lax.Precision.HIGHEST)
    values_new = jnp.dot(normed, w_value, precision=lax.Precision.HIGHEST)
    return (keys_new, values_new)


def shards(latents, pixel_keys, pixel_values, norm_gain, w_key, w_value, pixel_queries):
    top, total, weighted = partials(latents, pixel_keys, pixel_values)
    best = lax.pmax(top, "pix")
    rescale = jnp.exp(top - best)
    whole_total, whole_weighted = lax.psum((total * rescale, weighted * rescale[:, None]), "pix")
    latent_state = latents + whole_weighted / whole_total[:, None]
    latent_keys, latent_values = project(latent_state, norm_gain, w_key, w_value)
    ptop, ptotal, pweighted = partials(pixel_queries, latent_keys, latent_values)
    ptop, ptotal, pweighted = joined((ptop, ptotal, pweighted), "lat", combine_parts)
    pixel_out = pweighted / ptotal[:, None]
    return (latent_state, pixel_out)


def solution(mesh):
    in_specs = (P("lat", None), P("pix", None), P("pix", None), P(), P(), P(), P("pix", None))
    out_specs = (P("lat", None), P("pix", None))
    return jax.shard_map(shards, mesh=mesh, in_specs=in_specs, out_specs=out_specs, check_vma=False)
```

profile of v0, /device:TPU:0, one launch (start us, length us, event | category | flops | bytes accessed | tf_op | source)
XLA Modules:
  0.0 178.0 jit_solution(14502672150908622217)
XLA Ops:
  7.2 0.0 copy-start
  7.2 0.0 all-reduce.2.cloned.1.call-start
  7.2 1.2 copy-done
  8.4 3.1 %fusion.9 = (f32[512]{0:T(512)S(1)}, f32[512,512]{0,1:T(8,128)S(1)}) fusion(f32[512,512]{1,0:T(8,128)} %param.9, f32[512,512]{1,0:T(8,128)S(1)} %copy-done), kind=kOutput, calls=%fused_computation.28 | convolution fusion | flops 1611136512 | bytes 3147776 | tf_op jit(solution)/shard_map/dot_general | solution.py:16
  11.5 0.0 copy-start.1
  11.5 23.3 %pmax.7 = f32[512]{0:T(512)S(1)} all-reduce(f32[512]{0:T(512)S(1)} %get-tuple-element.66), channel_id=1, replica_groups=mesh['pix'=8,'lat'=4] {'pix'}, use_global_device_ids=true, to_apply=%region_1.0 | all-reduce | flops 512 | bytes 4096 | tf_op jit(solution)/shard_map/pmax | solution.py:44
  34.8 0.2 fusion.1
  35.0 0.0 copy-start.5
  35.0 4.1 %convolution_multiply_fusion.1 = f32[512,512]{1,0:T(8,128)} fusion(f32[512,512]{1,0:T(8,128)} %param.11, f32[512,512]{0,1:T(8,128)S(1)} %get-tuple-element.67, f32[512]{0:T(512)S(1)} %get-tuple-element.63, f32[512]{0:T(512)S(1)} %get-tuple-element.66), kind=kOutput, calls=%fused_computation.8 | convolution fusion | flops 1611137024 | bytes 3149824 | tf_op jit(solution)/shard_map/dot_general | solution.py:22
  39.1 0.0 all-reduce.2.cloned.1.call-update
  39.2 0.0 all-gather.7.cloned.1.call-start
  39.2 17.8 %psum.15 = f32[512]{0:T(512)S(1)} all-reduce(f32[512]{0:T(512)S(1)} %get-tuple-element.62), channel_id=1, replica_groups=mesh['pix'=8,'lat'=4] {'pix'}, use_global_device_ids=true, to_apply=%region_4.0 | all-reduce | flops 512 | bytes 4096 | tf_op jit(solution)/shard_map/psum | solution.py:46
  57.0 58.1 %all-reduce.2.cloned.1.call-done = f32[512,512]{1,0:T(8,128)} async-done(((f32[512,512]{1,0:T(8,128)}), f32[512,512]{1,0:T(8,128)}) %all-reduce.2.cloned.1.call-update) | async-done | bytes 1048592 | tf_op jit(solution)/shard_map/psum | solution.py:46
  115.1 0.0 copy-done.1
  115.1 0.0 copy-start.4
  115.1 1.6 multiply_reduce_fusion
  116.7 0.0 copy-start.2
  116.7 0.0 copy-done.5
  116.7 3.5 %fusion.6 = f32[512,512]{1,0:T(8,128)S(1)} fusion(f32[512,512]{1,0:T(8,128)} %param.14, f32[512,512]{1,0:T(8,128)S(1)} %get-tuple-element.61, f32[512]{0:T(512)S(1)} %copy-done.5, f32[512]{0:T(512)S(1)} %add_sqrt_fusion), kind=kOutput, calls=%fused_computation.21 | convolution fusion | flops 1611137024 | bytes 3149824 | tf_op jit(solution)/shard_map/dot_general | solution.py:38
  120.3 0.0 copy-done.2
  120.3 0.0 copy-done.4
  120.3 0.0 copy-start.3
  120.3 1.9 %fusion.7 = f32[512,512]{1,0:T(8,128)S(1)} fusion(f32[512,512]{1,0:T(8,128)S(1)} %copy-done.4, f32[512,512]{1,0:T(8,128)S(1)} %get-tuple-element.61, f32[512]{0:T(512)S(1)} %copy-done.5, f32[512]{0:T(512)S(1)} %add_sqrt_fusion), kind=kOutput, calls=%fused_computation.22 | convolution fusion | flops 1611137024 | bytes 3149824 | tf_op jit(solution)/shard_map/dot_general | solution.py:37
  122.2 0.0 copy-done.3
  122.3 2.0 %fusion.10 = (f32[512]{0:T(512)S(1)}, f32[512,512]{0,1:T(8,128)S(1)}) fusion(f32[512,512]{1,0:T(8,128)S(1)} %fusion.7, f32[512,512]{1,0:T(8,128)S(1)} %copy-done.3), kind=kOutput, calls=%fused_computation.29 | convolution fusion | flops 1611136512 | bytes 3147776 | tf_op jit(solution)/shard_map/dot_general | solution.py:16
  124.2 2.9 %fusion.2 = f32[512,512]{1,0:T(8,128)} fusion(f32[512,512]{1,0:T(8,128)S(1)} %fusion.6, f32[512,512]{0,1:T(8,128)S(1)} %get-tuple-element.69, f32[512]{0:T(512)S(1)} %get-tuple-element.68), kind=kOutput, calls=%fused_computation.16 | convolution fusion | flops 1610874880 | bytes 3147776 | tf_op jit(solution)/shard_map/dot_general | solution.py:22
  127.1 0.0 all-gather.7.cloned.1.call-update
  127.1 5.2 %all-gather.3 = f32[4,1,512]{2,1,0:T(1,128)S(1)} all-gather(f32[1,1,512]{2,1,0:T(1,128)S(1)} %bitcast.38), channel_id=2, replica_groups=mesh['pix'=8,'lat'=4] {'lat'}, dimensions={0}, use_global_device_ids=true | all-gather | bytes 10240 | tf_op jit(solution)/shard_map/all_gather | solution.py:8
  132.3 0.3 fusion.3
  132.6 5.2 %all-gather.4 = f32[4,1,512]{2,1,0:T(1,128)S(1)} all-gather(f32[1,1,512]{2,1,0:T(1,128)S(1)} %bitcast.39), channel_id=3, replica_groups=mesh['pix'=8,'lat'=4] {'lat'}, dimensions={0}, use_global_device_ids=true | all-gather | bytes 10240 | tf_op jit(solution)/shard_map/all_gather | solution.py:8
  137.8 23.5 %all-gather.7.cloned.1.call-done = f32[2048,512]{1,0:T(8,128)} async-done(((f32[512,512]{1,0:T(8,128)}), f32[2048,512]{1,0:T(8,128)}) %all-gather.7.cloned.1.call-update) | async-done | bytes 4194320 | tf_op jit(solution)/shard_map/all_gather | solution.py:8
  161.4 0.0 slice-start
  161.4 4.0 %slice.39 = f32[1536,512]{1,0:T(8,128)} slice(f32[2048,512]{1,0:T(8,128)} %all-gather.7.cloned.1.call-done), slice={[512:2048], [0:512]} | slice | bytes 6291456 | tf_op jit(solution)/shard_map/slice | solution.py:10
  165.3 0.0 slice-done
  165.3 4.7 %while.14 = (s32[]{:T(128)}, f32[512]{0:T(512)S(1)}, f32[512]{0:T(512)S(1)}, f32[512,512]{1,0:T(8,128)S(1)}, f32[3,512]{1,0:T(4,128)S(1)}, /*index=5*/f32[3,512]{1,0:T(4,128)S(1)}, f32[3,512,512]{2,1,0:T(8,128)}, s32[]{:T(128)}) while((s32[]{:T(128)}, f32[512]{0:T(512)S(1)}, f32[512]{0:T(512)S(1)}, f32[512,512]{1,0:T(8,128)S(1)}, ...), condition=%wide.region_9.10_spmd, body=%wide.region_8.9_spmd.sunk | while | flops 789506 | bytes 3174501 | solution.py:11
  165.4 1.5 fusion.20
  166.9 1.5 fusion.20
  168.5 1.5 fusion.20
  170.0 1.1 broadcast_divide_fusion
  (14 shorter events, 0.1 us)
Async XLA Ops:
  7.2 1.2 copy-start
  7.2 107.9 %all-reduce.2.cloned.1.call-start = ((), (), s32[]{:S(2)}) async-start(), calls=%async_computation | async-start | bytes 2097152 | tf_op jit(solution)/shard_map/psum | solution.py:46
  11.5 103.6 %copy-start.1 = (f32[512,512]{1,0:T(8,128)S(1)}, f32[512,512]{1,0:T(8,128)}, u32[]{:S(2)}) copy-start(f32[512,512]{1,0:T(8,128)} %param.9) | copy-start | bytes 3145732
  35.0 81.7 %copy-start.5 = (f32[512]{0:T(512)S(1)}, f32[512]{0:T(512)}, u32[]{:S(2)}) copy-start(f32[512]{0:T(512)} %param.12) | copy-start | bytes 6148
  39.2 122.2 %all-gather.7.cloned.1.call-start = ((), (), s32[]{:S(2)}) async-start(), calls=%async_computation.1 | async-start | bytes 5242880 | tf_op jit(solution)/shard_map/all_gather | solution.py:8
  115.1 5.2 %copy-start.4 = (f32[512,512]{1,0:T(8,128)S(1)}, f32[512,512]{1,0:T(8,128)}, u32[]{:S(2)}) copy-start(f32[512,512]{1,0:T(8,128)} %param.13) | copy-start | bytes 3145732
  116.7 3.6 %copy-start.2 = (f32[512,512]{1,0:T(8,128)}, f32[512,512]{1,0:T(8,128)S(1)}, u32[]{:S(2)}) copy-start(f32[512,512]{1,0:T(8,128)S(1)} %get-tuple-element.61) | copy-start | bytes 3145732
  120.3 2.0 %copy-start.3 = (f32[512,512]{1,0:T(8,128)S(1)}, f32[512,512]{1,0:T(8,128)}, u32[]{:S(2)}) copy-start(f32[512,512]{1,0:T(8,128)} %param.15) | copy-start | bytes 3145732
  161.4 4.0 %slice-start = ((f32[2048,512]{1,0:T(8,128)}), f32[512,512]{1,0:T(8,128)S(1)}, s32[]{:S(2)}) async-start(f32[2048,512]{1,0:T(8,128)} %all-gather.7.cloned.1.call-done), calls=%async_computation.2 | async-start | bytes 2097152 | tf_op jit(solution)/shard_map/slice | solution.py:9
Sparse Core Ops, SparseCore 0:
  39.3 75.7 all-reduce.1
  127.3 34.0 all-gather.6
where the time goes:
time: 178 us
  waiting for transfers between devices  81.6 us (46%)
  blocking collectives  51.5 us (29%)
  matrix products  17.5 us (10%)
  between operations  14.2 us (8%)
  other arithmetic  7.85 us (4%)
  local copies, waits for them, and re-layouts  5.2 us (3%)
    psum x1, waiting for transfers between devices, shards(): lax.psum((total * rescale, weighted * rescale[:, None]), 'pix')  58.1 us
    all_gather x1, waiting for transfers between devices, joined(): pieces = jax.tree.map(lambda part: lax.all_gather(part, axis), value)  23.5 us
    pmax x1, blocking collectives, shards(): best = lax.pmax(top, 'pix')  23.3 us
    psum x1, blocking collectives, shards(): lax.psum((total * rescale, weighted * rescale[:, None]), 'pix')  17.8 us
    all_gather x2, blocking collectives, joined(): pieces = jax.tree.map(lambda part: lax.all_gather(part, axis), value)  10.4 us
    dot_general x2, matrix products, partials(): weighted = jnp.dot(weights, values, precision=lax.Precision.HIGHEST)  7.04 us
    dot_general x2, matrix products, partials(): jnp.dot(queries, keys.T, precision=lax.Precision.HIGHEST)  5.05 us
    add x3, other arithmetic, combine_parts(): weighted = first[2] * scale_a[:, None] + second[2] * scale_b[:, None]  4.56 us
  transfers between devices with their start and end apart: 2, of which 2 were waited for; matrix products, arithmetic and copies ran while one was open for 0% of the time, Pallas kernels for 0%

commit v1 on v0

v1 whole, which is shorter than its diff:
```python
import functools

import jax
import jax.numpy as jnp
from jax import lax
from jax.experimental import pallas as pl
from jax.experimental.pallas import tpu as pltpu
from jax.sharding import PartitionSpec as P

STAT = 8
PARAMS = pltpu.CompilerParams(vmem_limit_bytes=24 * 1024 * 1024)
VMEM = pl.BlockSpec(memory_space=pltpu.VMEM)
SMEM = pl.BlockSpec(memory_space=pltpu.SMEM)


def split(x):
    hi = x.astype(jnp.bfloat16)
    lo = (x - hi.astype(jnp.float32)).astype(jnp.bfloat16)
    return hi, lo


def dot3(a, b, dims):
    (ah, al), (bh, bl) = a, b
    dot = functools.partial(
        lax.dot_general, dimension_numbers=(dims, ((), ())), preferred_element_type=jnp.float32
    )
    return dot(ah, bh) + (dot(ah, bl) + dot(al, bh))


NT = ((1,), (1,))
NN = ((1,), (0,))


def call(body, outs, specs, scratch=(), name=None):
    return pl.pallas_call(
        body,
        out_shape=tuple(jax.ShapeDtypeStruct(s, jnp.float32) for s in outs),
        in_specs=list(specs),
        out_specs=tuple(VMEM for _ in outs),
        scratch_shapes=list(scratch),
        compiler_params=PARAMS,
        name=name,
    )


def pack_stats(top, total):
    rows = top.shape[0]
    lane = lax.broadcasted_iota(jnp.int32, (rows, 128), 1)
    wide = jnp.where(lane == 0, top, jnp.where(lane == 1, total, 0.0))
    return wide.T[:STAT]


def unpack_stats(tile):
    rows = tile.shape[1]
    wide = jnp.concatenate([tile] * (128 // STAT), axis=0).T
    return wide[:, 0:1], wide[:, 1:2]


def attend(scores):
    top = jnp.max(scores, axis=1, keepdims=True)
    weights = jnp.exp(scores - top)
    return top, weights, jnp.sum(weights, axis=1, keepdims=True)


def merge(parts):
    top = functools.reduce(jnp.maximum, [p[0] for p in parts])
    total = weighted = None
    for t, s, w in parts:
        scale = jnp.exp(t - top)
        total = s * scale if total is None else total + s * scale
        weighted = w * scale if weighted is None else weighted + w * scale
    return top, total, weighted


def load_packed(ref, rows):
    top, total = unpack_stats(ref[rows:rows + STAT, :rows])
    return top, total, ref[:rows]


def store_packed(ref, rows, part):
    top, total, weighted = part
    ref[:rows] = weighted
    ref[rows:rows + STAT, :rows] = pack_stats(top, total)
    if rows < ref.shape[1]:
        ref[rows:rows + STAT, rows:] = jnp.zeros((STAT, ref.shape[1] - rows), jnp.float32)


def partial_kernel(rank, queries, keys, values, *rest, blocks, scale):
    outs, (acc, stats) = rest[:blocks], rest[blocks:]
    scores = dot3(split(queries[...] * scale), split(keys[...]), NT)
    top, weights, total = attend(scores)
    acc[...] = dot3(split(weights), split(values[...]), NN)
    lane = lax.broadcasted_iota(jnp.int32, stats.shape, 1)
    stats[...] = jnp.where(lane == 0, top, total)
    rows = queries.shape[0] // blocks
    for k in range(blocks):
        at = pl.multiple_of((rank[0] ^ k) * rows, rows)
        block = pl.ds(at, rows)
        st = stats[block, :]
        store_packed(outs[k], rows, (st[:, 0:1], st[:, 1:2], acc[block, :]))


def merge_kernel(*refs, rows):
    store_packed(refs[-1], rows, merge([load_packed(r, rows) for r in refs[:-1]]))


def state_kernel(rank, latents, *refs, rows):
    _, total, weighted = merge([load_packed(r, rows) for r in refs[:-1]])
    at = pl.multiple_of(rank[0] * rows, rows)
    refs[-1][...] = latents[pl.ds(at, rows), :] + weighted / total


def query_kernel(queries, w_key, out, *, scale):
    out[...] = dot3(split(queries[...] * scale), split(w_key[...]), NT)


def read_kernel(ranks, queries, gain, *refs, blocks, halves):
    states, state_out, outs = refs[:blocks], refs[blocks], refs[blocks + 1:blocks + 1 + halves]
    acc, stats = refs[blocks + 1 + halves:]
    rows = states[0].shape[0]
    for k in range(blocks):
        at = pl.multiple_of((ranks[0] ^ k) * rows, rows)
        state_out[pl.ds(at, rows), :] = states[k][...]
    state = state_out[...]
    normed = state / jnp.sqrt(jnp.mean(state * state, axis=1, keepdims=True) + 1e-06) * gain[...]
    parts = split(normed)
    scores = dot3(split(queries[...]), parts, NT)
    top, weights, total = attend(scores)
    acc[...] = dot3(split(weights), parts, NN)
    lane = lax.broadcasted_iota(jnp.int32, stats.shape, 1)
    stats[...] = jnp.where(lane == 0, top, total)
    rows = queries.shape[0] // halves
    for k in range(halves):
        at = pl.multiple_of((ranks[1] ^ k) * rows, rows)
        block = pl.ds(at, rows)
        st = stats[block, :]
        store_packed(outs[k], rows, (st[:, 0:1], st[:, 1:2], acc[block, :]))


def mean_kernel(*refs, rows):
    _, total, weighted = merge([load_packed(r, rows) for r in refs[:-1]])
    refs[-1][...] = weighted / total


def out_kernel(rank, w_value, *refs, halves):
    parts, out = refs[:halves], refs[halves]
    rows = parts[0].shape[0]
    weight = split(w_value[...])
    for k in range(halves):
        at = pl.multiple_of((rank[0] ^ k) * rows, rows)
        out[pl.ds(at, rows), :] = dot3(split(parts[k][...]), weight, NN)


def swap(value, axis, n, mask):
    return lax.ppermute(value, axis, [(i, i ^ mask) for i in range(n)])


def shards(latents, pixel_keys, pixel_values, norm_gain, w_key, w_value, pixel_queries, *, npix, nlat):
    depth = latents.shape[1]
    scale = depth ** -0.5
    pix, lat = lax.axis_index("pix"), lax.axis_index("lat")
    group = min(4, npix)
    rank = pix & (group - 1)
    outer = []
    step = group
    while step < npix:
        outer.append(step)
        step *= 2
    if outer and group == 4:
        outer[0] = 6
        rank = rank ^ jnp.where(pix & 4, 2, 0)
    rank = rank.reshape(1)
    rows = latents.shape[0] // group
    packed = (rows + STAT, depth)

    partials = call(
        functools.partial(partial_kernel, blocks=group, scale=scale),
        [packed] * group,
        [SMEM, VMEM, VMEM, VMEM],
        [pltpu.VMEM(latents.shape, jnp.float32), pltpu.VMEM((latents.shape[0], 128), jnp.float32)],
        "partial",
    )(rank, latents, pixel_keys, pixel_values)
    pieces = [partials[0]] + [swap(partials[k], "pix", npix, k) for k in range(group - 1, 0, -1)]

    projected, = call(
        functools.partial(query_kernel, scale=scale), [pixel_queries.shape], [VMEM, VMEM], (), "queries"
    )(pixel_queries, w_key)

    for mask in outer:
        merged, = call(
            functools.partial(merge_kernel, rows=rows), [packed], [VMEM] * len(pieces), (), "merge"
        )(*pieces)
        pieces = [merged, swap(merged, "pix", npix, mask)]
    state, = call(
        functools.partial(state_kernel, rows=rows), [(rows, depth)], [SMEM, VMEM] + [VMEM] * len(pieces), (), "state"
    )(rank, latents, *pieces)
    states = [state] + [swap(state, "pix", npix, k) for k in range(1, group)]

    halves = min(2, nlat)
    half = lat & (halves - 1)
    ranks = jnp.stack([rank[0], half])
    qrows = pixel_queries.shape[0] // halves
    packed = (qrows + STAT, depth)
    reads = call(
        functools.partial(read_kernel, blocks=group, halves=halves),
        [latents.shape] + [packed] * halves,
        [SMEM, VMEM, VMEM] + [VMEM] * group,
        [pltpu.VMEM(pixel_queries.shape, jnp.float32), pltpu.VMEM((pixel_queries.shape[0], 128), jnp.float32)],
        "read",
    )(ranks, projected, norm_gain.reshape(1, depth), *states)
    latent_state, reads = reads[0], reads[1:]
    pieces = [reads[0]] + [swap(reads[k], "lat", nlat, k) for k in range(1, halves)]
    step = halves
    while step < nlat:
        merged, = call(
            functools.partial(merge_kernel, rows=qrows), [packed], [VMEM] * len(pieces), (), "merge"
        )(*pieces)
        pieces = [merged, swap(merged, "lat", nlat, step)]
        step *= 2
    mean, = call(
        functools.partial(mean_kernel, rows=qrows), [(qrows, depth)], [VMEM] * len(pieces), (), "mean"
    )(*pieces)
    means = [mean] + [swap(mean, "lat", nlat, k) for k in range(1, halves)]
    pixel_out, = call(
        functools.partial(out_kernel, halves=halves), [pixel_queries.shape], [SMEM, VMEM] + [VMEM] * halves, (), "out"
    )(half.reshape(1), w_value, *means)
    return latent_state, pixel_out


def solution(mesh):
    body = functools.partial(shards, npix=mesh.shape["pix"], nlat=mesh.shape["lat"])
    in_specs = (P("lat", None), P("pix", None), P("pix", None), P(), P(), P(), P("pix", None))
    out_specs = (P("lat", None), P("pix", None))
    return jax.shard_map(body, mesh=mesh, in_specs=in_specs, out_specs=out_specs, check_vma=False)
```

time: 178 us -> 76.7 us (0.43)
  blocking collectives: 51.5 us -> 0 us
  waiting for transfers between devices: 81.6 us -> 45.1 us
  matrix products: 17.5 us -> 0 us
  starting transfers between devices: 0.08 us -> 17.4 us
  between operations: 14.2 us -> 0.73 us
  Pallas kernels: 0 us -> 9.55 us
  other arithmetic: 7.85 us -> 0.08 us
    psum x1 -> x0, waiting for transfers between devices: 58.1 us -> none  [shards(): lax.psum((total * rescale, weighted * rescale[:, None]), 'pix')]
    ppermute x0 -> x10, waiting for transfers between devices: none -> 45.1 us  [swap(): return lax.ppermute(value, axis, [(i, i ^ mask) for i in range(n)])]
    all_gather x1 -> x0, waiting for transfers between devices: 23.5 us -> none  [joined(): pieces = jax.tree.map(lambda part: lax.all_gather(part, axis), value)]
    pmax x1 -> x0, blocking collectives: 23.3 us -> none  [shards(): best = lax.pmax(top, 'pix')]
    psum x1 -> x0, blocking collectives: 17.8 us -> none  [shards(): lax.psum((total * rescale, weighted * rescale[:, None]), 'pix')]
    dot_general x6 -> x0, matrix products: 17.5 us -> none  [the longest x2 7.04 us: partials(): weighted = jnp.dot(weights, values, precision=lax.Precision.HIGHEST)]
    ppermute x0 -> x10, starting transfers between devices: none -> 17.4 us  [swap(): return lax.ppermute(value, axis, [(i, i ^ mask) for i in range(n)])]
    all_gather x2 -> x0, blocking collectives: 10.4 us -> none  [joined(): pieces = jax.tree.map(lambda part: lax.all_gather(part, axis), value)]
  transfers between devices with their start and end apart: 2 -> 10, of which waited for: 2 -> 9; matrix products, arithmetic and copies ran while one was open for 0% -> 0% of each run, Pallas kernels for 0% -> 1%
where the time goes in v1:
time: 76.7 us; the launch traced here: 76.5 us
  waiting for transfers between devices  45.1 us (59%)
  starting transfers between devices  17.4 us (23%)
  Pallas kernels  9.55 us (12%)
  local copies, waits for them, and re-layouts  3.69 us (5%)
    ppermute x10, waiting for transfers between devices, swap(): return lax.ppermute(value, axis, [(i, i ^ mask) for i in range(n)])  45.1 us
    ppermute x10, starting transfers between devices, swap(): return lax.ppermute(value, axis, [(i, i ^ mask) for i in range(n)])  17.4 us
    unnamed x16, local copies, waits for them, and re-layouts  3.69 us
    pallas_call x1, Pallas kernels, shards(): call(functools.partial(read_kernel, blocks=group, halves=halves), [latent...  2.85 us
    pallas_call x1, Pallas kernels, shards(): call(functools.partial(partial_kernel, blocks=group, scale=scale), [packe...  2.11 us
    pallas_call x1, Pallas kernels, shards(): call(functools.partial(out_kernel, halves=halves), [pixel_queries.shape],...  1.97 us
  transfers between devices with their start and end apart: 10, of which 9 were waited for; matrix products, arithmetic and copies ran while one was open for 0% of the time, Pallas kernels for 1%

profile of v1, /device:TPU:0, one launch (start us, length us, event | category | flops | bytes accessed | tf_op | source)
XLA Modules:
  0.0 76.5 jit_solution(3513356811521713687)
XLA Ops:
  0.6 0.0 copy-start
  0.7 1.2 %copy-done = f32[512,512]{1,0:T(8,128)S(1)} copy-done((f32[512,512]{1,0:T(8,128)S(1)}, f32[512,512]{1,0:T(8,128)}, u32[]{:S(2)}) %copy-start) | copy-done | bytes 1048600
  1.9 0.0 copy-start.4
  1.9 1.2 %copy-done.4 = f32[512,512]{1,0:T(8,128)S(1)} copy-done((f32[512,512]{1,0:T(8,128)S(1)}, f32[512,512]{1,0:T(8,128)}, u32[]{:S(2)}) %copy-start.4) | copy-done | bytes 1048600
  3.1 0.0 copy-start.5
  3.1 1.2 %copy-done.5 = f32[512,512]{1,0:T(8,128)S(1)} copy-done((f32[512,512]{1,0:T(8,128)S(1)}, f32[512,512]{1,0:T(8,128)}, u32[]{:S(2)}) %copy-start.5) | copy-done | bytes 1048600
  4.3 2.1 %partial.1 = (f32[136,512]{1,0:T(8,128)S(1)}, f32[136,512]{1,0:T(8,128)S(1)}, f32[136,512]{1,0:T(8,128)S(1)}, f32[136,512]{1,0:T(8,128)S(1)}) custom-call(s32[1]{0:T(128)} %bitcast.rank, f32[512,512]{1,0:T(8,128)S(1)} %copy-done, f32[512,512]{1,0:T(8,128)S(1)} %copy-done.4, f32[512,512]{1,0:T(8,128)S(1)} %copy-done.5), custom_call_target="tpu_custom_call" | custom-call | tf_op jit(solution)/shard_map/partial/pallas_call | solution.py:176
  6.4 0.0 copy-start.1
  6.5 4.1 %collective-permute-start = (f32[136,512]{1,0:T(8,128)S(1)}, f32[136,512]{1,0:T(8,128)S(1)}, u32[]{:S(2)}, u32[]{:S(2)}) collective-permute-start(f32[136,512]{1,0:T(8,128)S(1)} %get-tuple-element.10), channel_id=1, source_target_pairs={{0,12},{4,8},{8,4},{12,0},{16,28},{20,24},{24,20},{28,16},{1,13},{... | collective-permute-start | bytes 835592 | tf_op jit(solution)/shard_map/ppermute | solution.py:155
  10.5 0.5 collective-permute-start.1
  11.0 0.2 collective-permute-start.2
  11.2 6.9 %collective-permute-done.refs_1_ = f32[136,512]{1,0:T(8,128)S(1)} collective-permute-done((f32[136,512]{1,0:T(8,128)S(1)}, f32[136,512]{1,0:T(8,128)S(1)}, u32[]{:S(2)}, u32[]{:S(2)}) %collective-permute-start) | collective-permute-done | bytes 278560 | tf_op jit(solution)/shard_map/ppermute | solution.py:155
  18.1 5.3 %collective-permute-done.1.refs_2_ = f32[136,512]{1,0:T(8,128)S(1)} collective-permute-done((f32[136,512]{1,0:T(8,128)S(1)}, f32[136,512]{1,0:T(8,128)S(1)}, u32[]{:S(2)}, u32[]{:S(2)}) %collective-permute-start.1) | collective-permute-done | bytes 278560 | tf_op jit(solution)/shard_map/ppermute | solution.py:155
  23.4 0.0 collective-permute-done.2.refs_3_
  23.4 0.0 copy-start.3
  23.4 0.5 merge.2.refs_0_
  23.8 0.0 copy-start.2
  23.8 3.7 %collective-permute-start.3 = (f32[136,512]{1,0:T(8,128)S(1)}, f32[136,512]{1,0:T(8,128)S(1)}, u32[]{:S(2)}, u32[]{:S(2)}) collective-permute-start(f32[136,512]{1,0:T(8,128)S(1)} %merge.2.refs_0_), channel_id=1, source_target_pairs={{0,24},{4,28},{8,16},{12,20},{16,8},{20,12},{24,0},{28,4},{1,25},{... | collective-permute-start | bytes 835592 | tf_op jit(solution)/shard_map/ppermute | solution.py:155
  27.5 6.8 %collective-permute-done.3.refs_1_ = f32[136,512]{1,0:T(8,128)S(1)} collective-permute-done((f32[136,512]{1,0:T(8,128)S(1)}, f32[136,512]{1,0:T(8,128)S(1)}, u32[]{:S(2)}, u32[]{:S(2)}) %collective-permute-start.3) | collective-permute-done | bytes 278560 | tf_op jit(solution)/shard_map/ppermute | solution.py:155
  34.3 0.0 copy-done.1
  34.3 0.3 state.1.refs_0_
  34.6 6.6 %collective-permute-start.6 = (f32[128,512]{1,0:T(8,128)S(1)}, f32[128,512]{1,0:T(8,128)S(1)}, u32[]{:S(2)}, u32[]{:S(2)}) collective-permute-start(f32[128,512]{1,0:T(8,128)S(1)} %state.1.refs_0_), channel_id=1, source_target_pairs={{0,12},{4,8},{8,4},{12,0},{16,28},{20,24},{24,20},{28,16},{1,13},{... | collective-permute-start | bytes 786440 | tf_op jit(solution)/shard_map/ppermute | solution.py:155
  41.2 0.0 collective-permute-start.5
  41.2 0.6 collective-permute-start.4
  41.8 0.0 copy-done.3
  41.8 0.0 copy-done.2
  41.8 1.0 %queries.3 = f32[512,512]{1,0:T(8,128)S(1)} custom-call(f32[512,512]{1,0:T(8,128)S(1)} %copy-done.2, f32[512,512]{1,0:T(8,128)S(1)} %copy-done.3), custom_call_target="tpu_custom_call" | custom-call | tf_op jit(solution)/shard_map/queries/pallas_call | solution.py:185
  42.9 0.0 copy-start.7
  42.9 0.1 pad_add_fusion.ranks
  43.0 5.4 %collective-permute-done.6.refs_3_ = f32[128,512]{1,0:T(8,128)S(1)} collective-permute-done((f32[128,512]{1,0:T(8,128)S(1)}, f32[128,512]{1,0:T(8,128)S(1)}, u32[]{:S(2)}, u32[]{:S(2)}) %collective-permute-start.6) | collective-permute-done | bytes 262176 | tf_op jit(solution)/shard_map/ppermute | solution.py:155
  48.4 3.4 %collective-permute-done.5.refs_2_ = f32[128,512]{1,0:T(8,128)S(1)} collective-permute-done((f32[128,512]{1,0:T(8,128)S(1)}, f32[128,512]{1,0:T(8,128)S(1)}, u32[]{:S(2)}, u32[]{:S(2)}) %collective-permute-start.5) | collective-permute-done | bytes 262176 | tf_op jit(solution)/shard_map/ppermute | solution.py:155
  51.8 0.7 collective-permute-done.4.refs_1_
  52.5 0.0 copy-done.7
  52.5 2.8 %read.1 = (f32[512,512]{1,0:T(8,128)}, f32[264,512]{1,0:T(8,128)S(1)}, f32[264,512]{1,0:T(8,128)S(1)}) custom-call(s32[2]{0:T(128)S(1)} %pad_add_fusion.ranks, f32[512,512]{1,0:T(8,128)S(1)} %queries.3, f32[1,512]{1,0:T(1,128)S(1)} %bitcast.3, f32[128,512]{1,0:T(8,128)S(1)} %state.1.refs_0_, f32[128,512]{1,0:T(8,128)S(1)} %collective-permute-done.4.refs_1_, ...), custom_call_target="tpu_custom_call" | custom-call | tf_op jit(solution)/shard_map/read/pallas_call | solution.py:204
  55.3 0.1 collective-permute-start.7
  55.4 1.9 %collective-permute-done.7.refs_1_ = f32[264,512]{1,0:T(8,128)S(1)} collective-permute-done((f32[264,512]{1,0:T(8,128)S(1)}, f32[264,512]{1,0:T(8,128)S(1)}, u32[]{:S(2)}, u32[]{:S(2)}) %collective-permute-start.7) | collective-permute-done | bytes 540704 | tf_op jit(solution)/shard_map/ppermute | solution.py:155
  57.3 0.5 merge.3.refs_0_
  57.8 0.0 copy-start.6
  57.8 1.6 %collective-permute-start.8 = (f32[264,512]{1,0:T(8,128)S(1)}, f32[264,512]{1,0:T(8,128)S(1)}, u32[]{:S(2)}, u32[]{:S(2)}) collective-permute-start(f32[264,512]{1,0:T(8,128)S(1)} %merge.3.refs_0_), channel_id=1, source_target_pairs={{0,2},{1,3},{2,0},{3,1},{4,6},{5,7},{6,4},{7,5},{8,10},{9,11},{10,... | collective-permute-start | bytes 1622024 | tf_op jit(solution)/shard_map/ppermute | solution.py:155
  59.4 12.8 %collective-permute-done.8.refs_1_ = f32[264,512]{1,0:T(8,128)S(1)} collective-permute-done((f32[264,512]{1,0:T(8,128)S(1)}, f32[264,512]{1,0:T(8,128)S(1)}, u32[]{:S(2)}, u32[]{:S(2)}) %collective-permute-start.8) | collective-permute-done | bytes 540704 | tf_op jit(solution)/shard_map/ppermute | solution.py:155
  72.2 0.4 mean.1.refs_0_
  72.6 0.1 collective-permute-start.9
  72.6 1.9 %collective-permute-done.9.refs_1_ = f32[256,512]{1,0:T(8,128)S(1)} collective-permute-done((f32[256,512]{1,0:T(8,128)S(1)}, f32[256,512]{1,0:T(8,128)S(1)}, u32[]{:S(2)}, u32[]{:S(2)}) %collective-permute-start.9) | collective-permute-done | bytes 524320 | tf_op jit(solution)/shard_map/ppermute | solution.py:155
  74.5 0.0 copy-done.6
  74.5 2.0 %out.1 = f32[512,512]{1,0:T(8,128)} custom-call(s32[1]{0:T(128)} %bitcast.1.rank, f32[512,512]{1,0:T(8,128)S(1)} %copy-done.6, f32[256,512]{1,0:T(8,128)S(1)} %mean.1.refs_0_, f32[256,512]{1,0:T(8,128)S(1)} %collective-permute-done.9.refs_1_), custom_call_target="tpu_custom_call" | custom-call | tf_op jit(solution)/shard_map/out/pallas_call | solution.py:224
Async XLA Ops:
  0.6 1.2 %copy-start = (f32[512,512]{1,0:T(8,128)S(1)}, f32[512,512]{1,0:T(8,128)}, u32[]{:S(2)}) copy-start(f32[512,512]{1,0:T(8,128)} %latents.1) | copy-start | bytes 3145732
  1.9 1.2 %copy-start.4 = (f32[512,512]{1,0:T(8,128)S(1)}, f32[512,512]{1,0:T(8,128)}, u32[]{:S(2)}) copy-start(f32[512,512]{1,0:T(8,128)} %keys.1) | copy-start | bytes 3145732
  3.1 1.2 %copy-start.5 = (f32[512,512]{1,0:T(8,128)S(1)}, f32[512,512]{1,0:T(8,128)}, u32[]{:S(2)}) copy-start(f32[512,512]{1,0:T(8,128)} %values.1) | copy-start | bytes 3145732
  6.4 27.9 %copy-start.1 = (f32[512,512]{1,0:T(8,128)S(1)}, f32[512,512]{1,0:T(8,128)}, u32[]{:S(2)}) copy-start(f32[512,512]{1,0:T(8,128)} %latents.1) | copy-start | bytes 3145732
  6.5 11.6 %collective-permute-start = (f32[136,512]{1,0:T(8,128)S(1)}, f32[136,512]{1,0:T(8,128)S(1)}, u32[]{:S(2)}, u32[]{:S(2)}) collective-permute-start(f32[136,512]{1,0:T(8,128)S(1)} %get-tuple-element.10), channel_id=1, source_target_pairs={{0,12},{4,8},{8,4},{12,0},{16,28},{20,24},{24,20},{28,16},{1,13},{... | collective-permute-start | bytes 835592 | tf_op jit(solution)/shard_map/ppermute | solution.py:155
  10.5 12.8 %collective-permute-start.1 = (f32[136,512]{1,0:T(8,128)S(1)}, f32[136,512]{1,0:T(8,128)S(1)}, u32[]{:S(2)}, u32[]{:S(2)}) collective-permute-start(f32[136,512]{1,0:T(8,128)S(1)} %get-tuple-element.11), channel_id=1, source_target_pairs={{0,8},{4,12},{8,0},{12,4},{16,24},{20,28},{24,16},{28,20},{1,9},{5... | collective-permute-start | bytes 835592 | tf_op jit(solution)/shard_map/ppermute | solution.py:155
  11.0 12.4 %collective-permute-start.2 = (f32[136,512]{1,0:T(8,128)S(1)}, f32[136,512]{1,0:T(8,128)S(1)}, u32[]{:S(2)}, u32[]{:S(2)}) collective-permute-start(f32[136,512]{1,0:T(8,128)S(1)} %get-tuple-element.12), channel_id=1, source_target_pairs={{0,4},{4,0},{8,12},{12,8},{16,20},{20,16},{24,28},{28,24},{1,5},{5... | collective-permute-start | bytes 835592 | tf_op jit(solution)/shard_map/ppermute | solution.py:155
  23.4 18.5 %copy-start.3 = (f32[512,512]{1,0:T(8,128)S(1)}, f32[512,512]{1,0:T(8,128)}, u32[]{:S(2)}) copy-start(f32[512,512]{1,0:T(8,128)} %w_key.1) | copy-start | bytes 3145732
  23.8 18.0 %copy-start.2 = (f32[512,512]{1,0:T(8,128)S(1)}, f32[512,512]{1,0:T(8,128)}, u32[]{:S(2)}) copy-start(f32[512,512]{1,0:T(8,128)} %queries.4) | copy-start | bytes 3145732
  23.8 10.5 %collective-permute-start.3 = (f32[136,512]{1,0:T(8,128)S(1)}, f32[136,512]{1,0:T(8,128)S(1)}, u32[]{:S(2)}, u32[]{:S(2)}) collective-permute-start(f32[136,512]{1,0:T(8,128)S(1)} %merge.2.refs_0_), channel_id=1, source_target_pairs={{0,24},{4,28},{8,16},{12,20},{16,8},{20,12},{24,0},{28,4},{1,25},{... | collective-permute-start | bytes 835592 | tf_op jit(solution)/shard_map/ppermute | solution.py:155
  34.6 13.8 %collective-permute-start.6 = (f32[128,512]{1,0:T(8,128)S(1)}, f32[128,512]{1,0:T(8,128)S(1)}, u32[]{:S(2)}, u32[]{:S(2)}) collective-permute-start(f32[128,512]{1,0:T(8,128)S(1)} %state.1.refs_0_), channel_id=1, source_target_pairs={{0,12},{4,8},{8,4},{12,0},{16,28},{20,24},{24,20},{28,16},{1,13},{... | collective-permute-start | bytes 786440 | tf_op jit(solution)/shard_map/ppermute | solution.py:155
  41.2 10.6 %collective-permute-start.5 = (f32[128,512]{1,0:T(8,128)S(1)}, f32[128,512]{1,0:T(8,128)S(1)}, u32[]{:S(2)}, u32[]{:S(2)}) collective-permute-start(f32[128,512]{1,0:T(8,128)S(1)} %state.1.refs_0_), channel_id=1, source_target_pairs={{0,8},{4,12},{8,0},{12,4},{16,24},{20,28},{24,16},{28,20},{1,9},{5... | collective-permute-start | bytes 786440 | tf_op jit(solution)/shard_map/ppermute | solution.py:155
  41.2 11.3 %collective-permute-start.4 = (f32[128,512]{1,0:T(8,128)S(1)}, f32[128,512]{1,0:T(8,128)S(1)}, u32[]{:S(2)}, u32[]{:S(2)}) collective-permute-start(f32[128,512]{1,0:T(8,128)S(1)} %state.1.refs_0_), channel_id=1, source_target_pairs={{0,4},{4,0},{8,12},{12,8},{16,20},{20,16},{24,28},{28,24},{1,5},{5... | collective-permute-start | bytes 786440 | tf_op jit(solution)/shard_map/ppermute | solution.py:155
  42.9 9.6 %copy-start.7 = (f32[512]{0:T(512)S(1)}, f32[512]{0:T(512)}, u32[]{:S(2)}) copy-start(f32[512]{0:T(512)} %param.10) | copy-start | bytes 6148
  55.3 2.0 %collective-permute-start.7 = (f32[264,512]{1,0:T(8,128)S(1)}, f32[264,512]{1,0:T(8,128)S(1)}, u32[]{:S(2)}, u32[]{:S(2)}) collective-permute-start(f32[264,512]{1,0:T(8,128)S(1)} %get-tuple-element.15), channel_id=1, source_target_pairs={{0,1},{1,0},{2,3},{3,2},{4,5},{5,4},{6,7},{7,6},{8,9},{9,8},{10,11... | collective-permute-start | bytes 1622024 | tf_op jit(solution)/shard_map/ppermute | solution.py:155
  57.8 16.7 %copy-start.6 = (f32[512,512]{1,0:T(8,128)S(1)}, f32[512,512]{1,0:T(8,128)}, u32[]{:S(2)}) copy-start(f32[512,512]{1,0:T(8,128)} %w_value.1) | copy-start | bytes 3145732
  57.8 14.4 %collective-permute-start.8 = (f32[264,512]{1,0:T(8,128)S(1)}, f32[264,512]{1,0:T(8,128)S(1)}, u32[]{:S(2)}, u32[]{:S(2)}) collective-permute-start(f32[264,512]{1,0:T(8,128)S(1)} %merge.3.refs_0_), channel_id=1, source_target_pairs={{0,2},{1,3},{2,0},{3,1},{4,6},{5,7},{6,4},{7,5},{8,10},{9,11},{10,... | collective-permute-start | bytes 1622024 | tf_op jit(solution)/shard_map/ppermute | solution.py:155
  72.6 2.0 %collective-permute-start.9 = (f32[256,512]{1,0:T(8,128)S(1)}, f32[256,512]{1,0:T(8,128)S(1)}, u32[]{:S(2)}, u32[]{:S(2)}) collective-permute-start(f32[256,512]{1,0:T(8,128)S(1)} %mean.1.refs_0_), channel_id=1, source_target_pairs={{0,1},{1,0},{2,3},{3,2},{4,5},{5,4},{6,7},{7,6},{8,9},{9,8},{10,11... | collective-permute-start | bytes 1572872 | tf_op jit(solution)/shard_map/ppermute | solution.py:155

commit v2 on v1

v2 whole, which is shorter than its diff:
```python
import functools

import jax
import jax.numpy as jnp
from jax import lax
from jax.experimental import pallas as pl
from jax.experimental.pallas import tpu as pltpu
from jax.sharding import PartitionSpec as P


STAT = 8
CHUNKS = 2
F32, BF16 = jnp.float32, jnp.bfloat16
PARAMS = pltpu.CompilerParams(vmem_limit_bytes=24 * 1024 * 1024)
VMEM = pl.BlockSpec(memory_space=pltpu.VMEM)
SMEM = pl.BlockSpec(memory_space=pltpu.SMEM)
ANY = pl.BlockSpec(memory_space=pltpu.HBM)
NT = ((1,), (1,))
NN = ((1,), (0,))


def split(x):
    hi = x.astype(BF16)
    lo = (x - hi.astype(F32)).astype(BF16)
    return hi, lo


def dot3(a, b, dims):
    (ah, al), (bh, bl) = a, b
    dot = functools.partial(lax.dot_general, dimension_numbers=(dims, ((), ())), preferred_element_type=F32)
    return dot(ah, bh) + (dot(ah, bl) + dot(al, bh))


def call(body, outs, specs, scratch=(), out_specs=None):
    shapes = tuple(jax.ShapeDtypeStruct(*(s if isinstance(s[0], tuple) else (s, F32))) for s in outs)
    return pl.pallas_call(
        body,
        out_shape=shapes,
        in_specs=list(specs),
        out_specs=tuple(out_specs or [VMEM] * len(outs)),
        scratch_shapes=list(scratch),
        compiler_params=PARAMS,
    )


def pack_stats(top, total):
    rows = top.shape[0]
    lane = lax.broadcasted_iota(jnp.int32, (rows, 128), 1)
    wide = jnp.where(lane == 0, top, jnp.where(lane == 1, total, 0.0))
    return wide.T[:STAT]


def unpack_stats(tile):
    wide = jnp.concatenate([tile] * (128 // STAT), axis=0).T
    return wide[:, 0:1], wide[:, 1:2]


def attend(scores):
    top = jnp.max(scores, axis=1, keepdims=True)
    weights = jnp.exp(scores - top)
    return top, weights, jnp.sum(weights, axis=1, keepdims=True)


def merge(parts):
    top = functools.reduce(jnp.maximum, [p[0] for p in parts])
    total = weighted = None
    for t, s, w in parts:
        scale = jnp.exp(t - top)
        total = s * scale if total is None else total + s * scale
        weighted = w * scale if weighted is None else weighted + w * scale
    return top, total, weighted


def load_packed(ref, rows):
    top, total = unpack_stats(ref[rows:rows + STAT, :rows])
    return top, total, ref[:rows]


def store_packed(ref, rows, part):
    top, total, weighted = part
    ref[:rows] = weighted
    ref[rows:rows + STAT, :rows] = pack_stats(top, total)
    if rows < ref.shape[1]:
        ref[rows:rows + STAT, rows:] = jnp.zeros((STAT, ref.shape[1] - rows), F32)


def store_blocks(outs, part):
    top, total, weighted = part
    rows = top.shape[0] // len(outs)
    for k, out in enumerate(outs):
        at = slice(k * rows, (k + 1) * rows)
        store_packed(out, rows, (top[at], total[at], weighted[at]))


def partial_of(queries, keys, values, scale):
    top, weights, total = attend(dot3(split(queries * scale), keys, NT))
    return top, total, dot3(split(weights), values, NN)


def first_kernel(rank, latents, keys, values, *rest, blocks, scale):
    rest = list(rest)
    outs = [rest.pop(0) for _ in range(blocks)]
    chunks = [rest.pop(0) for _ in range(CHUNKS)]
    kh, kl, vh, vl, kbuf, vbuf, qsem, ksem, vsem = rest
    rows = chunks[0].shape[0] // blocks

    def query_copies(a):
        copies = []
        for k in range(blocks):
            at = pl.multiple_of((rank[0] ^ k) * (rows * CHUNKS) + a * rows, 8)
            copies.append(pltpu.make_async_copy(
                latents.at[pl.ds(at, rows), :], chunks[a].at[pl.ds(k * rows, rows), :], qsem.at[a, k]))
        return copies

    pieces = ksem.shape[0]
    size = kbuf.shape[0] // pieces

    def copies_of(src, dst, sem):
        return [pltpu.make_async_copy(src.at[pl.ds(i * size, size), :], dst.at[pl.ds(i * size, size), :], sem.at[i])
                for i in range(pieces)]

    queries = [query_copies(a) for a in range(CHUNKS)]
    key_copies, value_copies = copies_of(keys, kbuf, ksem), copies_of(values, vbuf, vsem)
    for copy in queries[0] + key_copies + value_copies + sum(queries[1:], []):
        copy.start()
    for copy in queries[0] + key_copies:
        copy.wait()
    kh[...], kl[...] = split(kbuf[...])
    top, weights, total = attend(dot3(split(chunks[0][...] * scale), (kh[...], kl[...]), NT))
    for copy in value_copies:
        copy.wait()
    vh[...], vl[...] = split(vbuf[...])
    store_blocks(outs, (top, total, dot3(split(weights), (vh[...], vl[...]), NN)))
    for copy in sum(queries[1:], []):
        copy.wait()


def partial_kernel(queries, kh, kl, vh, vl, *outs, scale):
    store_blocks(outs, partial_of(queries[...], (kh[...], kl[...]), (vh[...], vl[...]), scale))


def merge_kernel(*refs, rows):
    store_packed(refs[-1], rows, merge([load_packed(r, rows) for r in refs[:-1]]))


def state_kernel(latents, *refs, rows):
    _, total, weighted = merge([load_packed(r, rows) for r in refs[:-1]])
    refs[-1][...] = latents[:rows] + weighted / total


def query_kernel(half, queries, w_key, *outs, halves, scale):
    weight = split(w_key[...])
    rows = queries.shape[0] // halves // CHUNKS
    for b in range(CHUNKS):
        picked = []
        for k in range(halves):
            at = pl.multiple_of((half[0] ^ k) * (rows * CHUNKS) + b * rows, 8)
            picked.append(queries[pl.ds(at, rows), :])
        hi, lo = split(dot3(split(jnp.concatenate(picked, axis=0) * scale), weight, NT))
        outs[2 * b][...] = hi
        outs[2 * b + 1][...] = lo


def normed_of(states, gain):
    state = jnp.concatenate([s[...] for s in states], axis=0)
    return state / jnp.sqrt(jnp.mean(state * state, axis=1, keepdims=True) + 1e-06) * gain[...]


def early_kernel(gain, *refs, blocks):
    queries, states, outs = refs[:2 * CHUNKS], refs[2 * CHUNKS:2 * CHUNKS + blocks], refs[2 * CHUNKS + blocks:]
    normed = split(normed_of(states, gain))
    for b in range(CHUNKS):
        top, weights, total = attend(dot3((queries[2 * b][...], queries[2 * b + 1][...]), normed, NT))
        outs[2 * b][...] = dot3(split(weights), normed, NN)
        lane = lax.broadcasted_iota(jnp.int32, outs[2 * b + 1].shape, 1)
        outs[2 * b + 1][...] = jnp.where(lane == 0, top, total)


def late_kernel(gain, qh, ql, acc, stats, *refs, blocks, halves):
    states, outs = refs[:blocks], refs[blocks:]
    normed = split(normed_of(states, gain))
    scores = dot3((qh[...], ql[...]), normed, NT)
    before, before_total = stats[:, 0:1], stats[:, 1:2]
    top = jnp.maximum(before, jnp.max(scores, axis=1, keepdims=True))
    weights = jnp.exp(scores - top)
    keep = jnp.exp(before - top)
    total = before_total * keep + jnp.sum(weights, axis=1, keepdims=True)
    store_blocks(outs, (top, total, acc[...] * keep + dot3(split(weights), normed, NN)))


def mean_kernel(*refs, rows):
    _, total, weighted = merge([load_packed(r, rows) for r in refs[:-1]])
    refs[-1][...] = weighted / total


def mean_state_kernel(rank, *refs, rows, parts, blocks):
    pieces, states = refs[:parts], refs[parts:parts + blocks * CHUNKS]
    out, state_out, sems = refs[parts + blocks * CHUNKS:]
    size = states[0].shape[0]
    copies = []
    for a in range(CHUNKS):
        for k in range(blocks):
            at = pl.multiple_of((rank[0] ^ k) * (size * CHUNKS) + a * size, 8)
            copies.append(pltpu.make_async_copy(
                states[a * blocks + k], state_out.at[pl.ds(at, size), :], sems.at[a, k]))
    for copy in copies:
        copy.start()
    mean_kernel(*pieces, out, rows=rows)
    for copy in copies:
        copy.wait()


def project_kernel(w_value, *refs):
    weight = split(w_value[...])
    half = len(refs) // 2
    for src, dst in zip(refs[:half], refs[half:]):
        dst[...] = dot3(split(src[...]), weight, NN)


def out_kernel(half, w_value, *refs, halves):
    ready, last = refs[:halves * (CHUNKS - 1)], refs[halves * (CHUNKS - 1):halves * CHUNKS]
    out, buf, sems = refs[halves * CHUNKS:]
    rows = last[0].shape[0]

    def copy_out(src, b, k):
        at = pl.multiple_of((half[0] ^ k) * (rows * CHUNKS) + b * rows, 8)
        return pltpu.make_async_copy(src, out.at[pl.ds(at, rows), :], sems.at[b, k])

    copies = [copy_out(ready[b * halves + k], b, k) for b in range(CHUNKS - 1) for k in range(halves)]
    for copy in copies:
        copy.start()
    weight = split(w_value[...])
    for k in range(halves):
        buf[pl.ds(k * rows, rows), :] = dot3(split(last[k][...]), weight, NN)
        copies.append(copy_out(buf.at[pl.ds(k * rows, rows), :], CHUNKS - 1, k))
        copies[-1].start()
    for copy in copies:
        copy.wait()


def swap(value, axis, n, mask):
    return lax.ppermute(value, axis, [(i, i ^ mask) for i in range(n)])


def shards(latents, pixel_keys, pixel_values, norm_gain, w_key, w_value, pixel_queries, *, npix, nlat):
    return window(latents, pixel_keys, pixel_values, norm_gain, w_key, w_value, pixel_queries, npix, nlat)


def window(latents, pixel_keys, pixel_values, norm_gain, w_key, w_value, pixel_queries, npix, nlat):
    depth = latents.shape[1]
    scale = depth ** -0.5
    pix, lat = lax.axis_index("pix"), lax.axis_index("lat")
    group = min(4, npix)
    rank = pix & (group - 1)
    outer = []
    step = group
    while step < npix:
        outer.append(step)
        step *= 2
    if outer and group == 4:
        outer[0] = 6
        rank = rank ^ jnp.where(pix & 4, 2, 0)
    rank = rank.reshape(1)
    halves = min(2, nlat)
    half = (lat & (halves - 1)).reshape(1)

    rows = latents.shape[0] // group // CHUNKS
    packed = (rows + STAT, depth)
    chunk = (latents.shape[0] // CHUNKS, depth)
    keys_shape = pixel_keys.shape
    first = call(
        functools.partial(first_kernel, blocks=group, scale=scale),
        [packed] * group + [chunk] * CHUNKS + [(keys_shape, BF16)] * 4,
        [SMEM, ANY, ANY, ANY],
        [pltpu.VMEM(keys_shape, F32), pltpu.VMEM(keys_shape, F32), pltpu.SemaphoreType.DMA((CHUNKS, group)),
         pltpu.SemaphoreType.DMA((4,)), pltpu.SemaphoreType.DMA((4,))])(rank, *[pltpu.with_memory_space_constraint(x, pltpu.HBM) for x in (latents, pixel_keys, pixel_values)])
    latent_chunks = first[group:group + CHUNKS]
    operands = first[group + CHUNKS:]
    partials = [first[:group]]
    for a in range(1, CHUNKS):
        partials.append(call(
            functools.partial(partial_kernel, scale=scale), [packed] * group, [VMEM] * 5, ())(latent_chunks[a], *operands))

    pieces = [[part[0]] + [swap(part[k], "pix", npix, k) for k in range(group - 1, 0, -1)]
              for part in partials]
    queries = call(
        functools.partial(query_kernel, halves=halves, scale=scale),
        [((pixel_queries.shape[0] // CHUNKS, depth), BF16)] * (2 * CHUNKS),
        [SMEM, VMEM, VMEM], ())(half, pixel_queries, w_key)

    for mask in outer:
        for a in range(CHUNKS):
            merged, = call(
                functools.partial(merge_kernel, rows=rows), [packed], [VMEM] * len(pieces[a]), ())(*pieces[a])
            pieces[a] = [merged, swap(merged, "pix", npix, mask)]
    states = []
    for a in range(CHUNKS):
        state, = call(
            functools.partial(state_kernel, rows=rows), [(rows, depth)], [VMEM] * (1 + len(pieces[a])), ())(latent_chunks[a], *pieces[a])
        states.append([state] + [swap(state, "pix", npix, k) for k in range(1, group)])

    gain = norm_gain.reshape(1, depth)
    qchunk = pixel_queries.shape[0] // CHUNKS
    qrows = qchunk // halves
    early = call(
        functools.partial(early_kernel, blocks=group),
        [(qchunk, depth), (qchunk, 128)] * CHUNKS, [VMEM] * (1 + 2 * CHUNKS + group), ())(gain, *queries, *states[0])
    packed = (qrows + STAT, depth)
    pieces = []
    for b in range(CHUNKS):
        late = call(
            functools.partial(late_kernel, blocks=group, halves=halves),
            [packed] * halves, [VMEM] * (5 + group), ())(gain, queries[2 * b], queries[2 * b + 1], early[2 * b], early[2 * b + 1], *states[1])
        pieces.append([late[0]] + [swap(late[k], "lat", nlat, k) for k in range(1, halves)])
    step = halves
    while step < nlat:
        for b in range(CHUNKS):
            merged, = call(
                functools.partial(merge_kernel, rows=qrows), [packed], [VMEM] * len(pieces[b]), ())(*pieces[b])
            pieces[b] = [merged, swap(merged, "lat", nlat, step)]
        step *= 2
    means = []
    for b in range(CHUNKS):
        if b == 0:
            mean, latent_state = call(
                functools.partial(mean_state_kernel, rows=qrows, parts=len(pieces[b]), blocks=group),
                [(qrows, depth), latents.shape], [SMEM] + [VMEM] * (len(pieces[b]) + group * CHUNKS),
                [pltpu.SemaphoreType.DMA((CHUNKS, group))], [VMEM, ANY])(rank, *pieces[b], *sum(states, []))
        else:
            mean, = call(
                functools.partial(mean_kernel, rows=qrows), [(qrows, depth)], [VMEM] * len(pieces[b]), ())(*pieces[b])
        means.append([mean] + [swap(mean, "lat", nlat, k) for k in range(1, halves)])
    ready = []
    for b in range(CHUNKS - 1):
        ready += call(
            project_kernel, [(qrows, depth)] * halves, [VMEM] * (1 + halves), ())(w_value, *means[b])
    pixel_out, = call(
        functools.partial(out_kernel, halves=halves), [pixel_queries.shape],
        [SMEM, VMEM] + [VMEM] * (halves * CHUNKS),
        [pltpu.VMEM((halves * qrows, depth), F32), pltpu.SemaphoreType.DMA((CHUNKS, halves))],
        [ANY])(half, w_value, *ready, *means[-1])
    return latent_state, pixel_out


def solution(mesh):
    body = functools.partial(shards, npix=mesh.shape["pix"], nlat=mesh.shape["lat"])
    in_specs = (P("lat", None), P("pix", None), P("pix", None), P(), P(), P(), P("pix", None))
    out_specs = (P("lat", None), P("pix", None))
    return jax.shard_map(body, mesh=mesh, in_specs=in_specs, out_specs=out_specs, check_vma=False)
```

time: 76.7 us -> 65.8 us (0.86)
  waiting for transfers between devices: 45.1 us -> 18.1 us
  starting transfers between devices: 17.4 us -> 30.2 us
  Pallas kernels: 9.55 us -> 15.7 us
  local copies, waits for them, and re-layouts: 3.69 us -> 0.7 us
    ppermute x10 -> x20, waiting for transfers between devices: 45.1 us -> 18.1 us  [swap(): return lax.ppermute(value, axis, [(i, i ^ mask) for i in range(n)])]
    ppermute x10 -> x20, starting transfers between devices: 17.4 us -> 30.2 us  [swap(): return lax.ppermute(value, axis, [(i, i ^ mask) for i in range(n)])]
    pallas_call x8 -> x16, Pallas kernels: 9.55 us -> 15.7 us  [the longest x1 3.37 us: window(): call(functools.partial(first_kernel, blocks=group, scale=scale), [packed]...]
    unnamed x16 -> x8, local copies, waits for them, and re-layouts: 3.69 us -> 0.7 us
  transfers between devices with their start and end apart: 10 -> 20, of which waited for: 9 -> 8; matrix products, arithmetic and copies ran while one was open for 0% -> 0% of each run, Pallas kernels for 1% -> 15%
where the time goes in v2:
time: 65.8 us; the launch traced here: 65.6 us
  starting transfers between devices  30.2 us (46%)
  waiting for transfers between devices  18.1 us (28%)
  Pallas kernels  15.7 us (24%)
  between operations  0.82 us (1%)
  local copies, waits for them, and re-layouts  0.7 us (1%)
    ppermute x20, starting transfers between devices, swap(): return lax.ppermute(value, axis, [(i, i ^ mask) for i in range(n)])  30.2 us
    ppermute x20, waiting for transfers between devices, swap(): return lax.ppermute(value, axis, [(i, i ^ mask) for i in range(n)])  18.1 us
    pallas_call x1, Pallas kernels, window(): call(functools.partial(first_kernel, blocks=group, scale=scale), [packed]...  3.37 us
    pallas_call x2, Pallas kernels, window(): call(functools.partial(late_kernel, blocks=group, halves=halves), [packed...  2.83 us
    pallas_call x1, Pallas kernels, window(): call(functools.partial(early_kernel, blocks=group), [(qchunk, depth), (qc...  2.18 us
    pallas_call x1, Pallas kernels, window(): call(functools.partial(out_kernel, halves=halves), [pixel_queries.shape],...  1.37 us
  transfers between devices with their start and end apart: 20, of which 8 were waited for; matrix products, arithmetic and copies ran while one was open for 0% of the time, Pallas kernels for 15%

profile of v2, /device:TPU:0, one launch (start us, length us, event | category | flops | bytes accessed | tf_op | source)
XLA Modules:
  0.0 65.6 jit_solution(14552550225018402216)
XLA Ops:
  0.6 3.4 %shard_map.87 = (f32[72,512]{1,0:T(8,128)S(1)}, f32[72,512]{1,0:T(8,128)S(1)}, f32[72,512]{1,0:T(8,128)S(1)}, f32[72,512]{1,0:T(8,128)S(1)}, f32[256,512]{1,0:T(...) custom-call(s32[1]{0:T(128)} %bitcast.rank, ...), custom_call_target="tpu_custom_call" | custom-call | tf_op jit(solution)/shard_map/pallas_call | solution.py:271
  4.0 4.1 %collective-permute-start = (f32[72,512]{1,0:T(8,128)S(1)}, f32[72,512]{1,0:T(8,128)S(1)}, u32[]{:S(2)}, u32[]{:S(2)}) collective-permute-start(f32[72,512]{1,0:T(8,128)S(1)} %get-tuple-element.38), channel_id=1, source_target_pairs={{0,12},{4,8},{8,4},{12,0},{16,28},{20,24},{24,20},{28,16},{1,13},{... | collective-permute-start | bytes 442376 | tf_op jit(solution)/shard_map/ppermute | solution.py:242
  8.1 0.4 collective-permute-start.1
  8.5 0.2 collective-permute-start.2
  8.7 1.2 %shard_map.91 = (f32[72,512]{1,0:T(8,128)S(1)}, f32[72,512]{1,0:T(8,128)S(1)}, f32[72,512]{1,0:T(8,128)S(1)}, f32[72,512]{1,0:T(8,128)S(1)}) custom-call(f32[256,512]{1,0:T(8,128)S(1)} %get-tuple-element.43.queries.latents, bf16[512,512]{1,0:T(8,128)(2,1)S(1)} %get-tuple-element.44.kh, bf16[512,512]{1,0:T(8,128)(2,1)S(1)} %get-tuple-element.45.kl, ...), custom_call_target="tpu_custom_call" | custom-call | tf_op jit(solution)/shard_map/pallas_call | solution.py:281
  9.9 2.9 %collective-permute-start.7 = (f32[72,512]{1,0:T(8,128)S(1)}, f32[72,512]{1,0:T(8,128)S(1)}, u32[]{:S(2)}, u32[]{:S(2)}) collective-permute-start(f32[72,512]{1,0:T(8,128)S(1)} %get-tuple-element.49), channel_id=1, source_target_pairs={{0,12},{4,8},{8,4},{12,0},{16,28},{20,24},{24,20},{28,16},{1,13},{... | collective-permute-start | bytes 442376 | tf_op jit(solution)/shard_map/ppermute | solution.py:242
  12.8 0.4 collective-permute-start.8
  13.3 0.0 collective-permute-done.refs_1_
  13.3 1.4 %collective-permute-start.9 = (f32[72,512]{1,0:T(8,128)S(1)}, f32[72,512]{1,0:T(8,128)S(1)}, u32[]{:S(2)}, u32[]{:S(2)}) collective-permute-start(f32[72,512]{1,0:T(8,128)S(1)} %get-tuple-element.51), channel_id=1, source_target_pairs={{0,4},{4,0},{8,12},{12,8},{16,20},{20,16},{24,28},{28,24},{1,5},{5... | collective-permute-start | bytes 442376 | tf_op jit(solution)/shard_map/ppermute | solution.py:242
  14.7 1.7 %collective-permute-done.1.refs_2_ = f32[72,512]{1,0:T(8,128)S(1)} collective-permute-done((f32[72,512]{1,0:T(8,128)S(1)}, f32[72,512]{1,0:T(8,128)S(1)}, u32[]{:S(2)}, u32[]{:S(2)}) %collective-permute-start.1) | collective-permute-done | bytes 147488 | tf_op jit(solution)/shard_map/ppermute | solution.py:242
  16.4 2.0 %collective-permute-done.2.refs_3_ = f32[72,512]{1,0:T(8,128)S(1)} collective-permute-done((f32[72,512]{1,0:T(8,128)S(1)}, f32[72,512]{1,0:T(8,128)S(1)}, u32[]{:S(2)}, u32[]{:S(2)}) %collective-permute-start.2) | collective-permute-done | bytes 147488 | tf_op jit(solution)/shard_map/ppermute | solution.py:242
  18.4 0.4 shard_map.88.refs_0_
  18.7 3.7 %collective-permute-start.3 = (f32[72,512]{1,0:T(8,128)S(1)}, f32[72,512]{1,0:T(8,128)S(1)}, u32[]{:S(2)}, u32[]{:S(2)}) collective-permute-start(f32[72,512]{1,0:T(8,128)S(1)} %shard_map.88.refs_0_), channel_id=1, source_target_pairs={{0,24},{4,28},{8,16},{12,20},{16,8},{20,12},{24,0},{28,4},{1,25},{... | collective-permute-start | bytes 442376 | tf_op jit(solution)/shard_map/ppermute | solution.py:242
  22.4 0.0 collective-permute-done.7.refs_1_
  22.4 0.0 copy-start.2
  22.4 0.4 shard_map.92.refs_0_
  22.8 4.4 %collective-permute-start.10 = (f32[72,512]{1,0:T(8,128)S(1)}, f32[72,512]{1,0:T(8,128)S(1)}, u32[]{:S(2)}, u32[]{:S(2)}) collective-permute-start(f32[72,512]{1,0:T(8,128)S(1)} %shard_map.92.refs_0_), channel_id=1, source_target_pairs={{0,24},{4,28},{8,16},{12,20},{16,8},{20,12},{24,0},{28,4},{1,25},{... | collective-permute-start | bytes 442376 | tf_op jit(solution)/shard_map/ppermute | solution.py:242
  27.2 0.6 collective-permute-done.3.refs_1_
  27.8 0.2 shard_map.89.refs_4_.refs_2_
  28.0 0.1 collective-permute-start.4
  28.1 4.7 %collective-permute-start.5 = (f32[64,512]{1,0:T(8,128)S(1)}, f32[64,512]{1,0:T(8,128)S(1)}, u32[]{:S(2)}, u32[]{:S(2)}) collective-permute-start(f32[64,512]{1,0:T(8,128)S(1)} %shard_map.89.refs_4_.refs_2_), channel_id=1, source_target_pairs={{0,8},{4,12},{8,0},{12,4},{16,24},{20,28},{24,16},{28,20},{1,9},{5... | collective-permute-start | bytes 393224 | tf_op jit(solution)/shard_map/ppermute | solution.py:242
  32.8 1.2 %collective-permute-start.6 = (f32[64,512]{1,0:T(8,128)S(1)}, f32[64,512]{1,0:T(8,128)S(1)}, u32[]{:S(2)}, u32[]{:S(2)}) collective-permute-start(f32[64,512]{1,0:T(8,128)S(1)} %shard_map.89.refs_4_.refs_2_), channel_id=1, source_target_pairs={{0,12},{4,8},{8,4},{12,0},{16,28},{20,24},{24,20},{28,16},{1,13},{... | collective-permute-start | bytes 393224 | tf_op jit(solution)/shard_map/ppermute | solution.py:242
  34.0 0.2 shard_map.93.refs_0_.refs_6_
  34.2 0.6 collective-permute-start.11
  34.9 1.7 %collective-permute-start.12 = (f32[64,512]{1,0:T(8,128)S(1)}, f32[64,512]{1,0:T(8,128)S(1)}, u32[]{:S(2)}, u32[]{:S(2)}) collective-permute-start(f32[64,512]{1,0:T(8,128)S(1)} %shard_map.93.refs_0_.refs_6_), channel_id=1, source_target_pairs={{0,8},{4,12},{8,0},{12,4},{16,24},{20,28},{24,16},{28,20},{1,9},{5... | collective-permute-start | bytes 393224 | tf_op jit(solution)/shard_map/ppermute | solution.py:242
  36.6 1.2 %collective-permute-start.13 = (f32[64,512]{1,0:T(8,128)S(1)}, f32[64,512]{1,0:T(8,128)S(1)}, u32[]{:S(2)}, u32[]{:S(2)}) collective-permute-start(f32[64,512]{1,0:T(8,128)S(1)} %shard_map.93.refs_0_.refs_6_), channel_id=1, source_target_pairs={{0,12},{4,8},{8,4},{12,0},{16,28},{20,24},{24,20},{28,16},{1,13},{... | collective-permute-start | bytes 393224 | tf_op jit(solution)/shard_map/ppermute | solution.py:242
  37.8 1.0 %shard_map.86 = (bf16[256,512]{1,0:T(8,128)(2,1)S(1)}, bf16[256,512]{1,0:T(8,128)(2,1)S(1)}, bf16[256,512]{1,0:T(8,128)(2,1)S(1)}, bf16[256,512]{1,0:T(8,128)(2,1)S(1)}) custom-call(s32[1]{0:T(128)} %bitcast.2.half, f32[512,512]{1,0:T(8,128)S(1)} %copy-done.1, f32[512,512]{1,0:T(8,128)S(1)} %copy-done.2), custom_call_target="tpu_custom_call" | custom-call | tf_op jit(solution)/shard_map/pallas_call | solution.py:286
  38.9 1.7 %collective-permute-done.6.refs_7_.refs_5_ = f32[64,512]{1,0:T(8,128)S(1)} collective-permute-done((f32[64,512]{1,0:T(8,128)S(1)}, f32[64,512]{1,0:T(8,128)S(1)}, u32[]{:S(2)}, u32[]{:S(2)}) %collective-permute-start.6) | collective-permute-done | bytes 131104 | tf_op jit(solution)/shard_map/ppermute | solution.py:242
  40.5 0.7 %copy-done.3 = f32[512]{0:T(512)S(1)} copy-done((f32[512]{0:T(512)S(1)}, f32[512]{0:T(512)}, u32[]{:S(2)}) %copy-start.3) | copy-done | bytes 2072
  41.2 2.2 %shard_map.90 = (f32[256,512]{1,0:T(8,128)S(1)}, f32[256,128]{1,0:T(8,128)S(1)}, f32[256,512]{1,0:T(8,128)S(1)}, f32[256,128]{1,0:T(8,128)S(1)}) custom-call(f32[1,512]{1,0:T(1,128)S(1)} %bitcast.3, bf16[256,512]{1,0:T(8,128)(2,1)S(1)} %get-tuple-element.32.refs_0_.qh, bf16[256,512]{1,0:T(8,128)(2,1)S(1)} %get-tuple-element.33.refs_1_.ql, ...), custom_call_target="tpu_custom_call" | custom-call | tf_op jit(solution)/shard_map/pallas_call | solution.py:305
  43.4 0.6 collective-permute-done.13.refs_3_.refs_9_
  44.0 1.4 %shard_map.94 = (f32[136,512]{1,0:T(8,128)S(1)}, f32[136,512]{1,0:T(8,128)S(1)}) custom-call(f32[1,512]{1,0:T(1,128)S(1)} %bitcast.4, bf16[256,512]{1,0:T(8,128)(2,1)S(1)} %get-tuple-element.32.refs_0_.qh, bf16[256,512]{1,0:T(8,128)(2,1)S(1)} %get-tuple-element.33.refs_1_.ql, f32[256,512]{1,0:T(8,128)S(1)} %get-tuple-element.41.acc, ...), custom_call_target="tpu_custom_call" | custom-call | tf_op jit(solution)/shard_map/pallas_call | solution.py:311
  45.4 0.1 collective-permute-start.14
  45.5 1.4 %shard_map.98 = (f32[136,512]{1,0:T(8,128)S(1)}, f32[136,512]{1,0:T(8,128)S(1)}) custom-call(f32[1,512]{1,0:T(1,128)S(1)} %bitcast.5, bf16[256,512]{1,0:T(8,128)(2,1)S(1)} %get-tuple-element.34.refs_2_.qh, bf16[256,512]{1,0:T(8,128)(2,1)S(1)} %get-tuple-element.35.refs_3_.ql, f32[256,512]{1,0:T(8,128)S(1)} %get-tuple-element.58.acc, ...), custom_call_target="tpu_custom_call" | custom-call | tf_op jit(solution)/shard_map/pallas_call | solution.py:311
  46.9 0.6 collective-permute-start.17
  47.5 0.3 shard_map.95.refs_0_
  47.8 1.5 %collective-permute-start.15 = (f32[136,512]{1,0:T(8,128)S(1)}, f32[136,512]{1,0:T(8,128)S(1)}, u32[]{:S(2)}, u32[]{:S(2)}) collective-permute-start(f32[136,512]{1,0:T(8,128)S(1)} %shard_map.95.refs_0_), channel_id=1, source_target_pairs={{0,2},{1,3},{2,0},{3,1},{4,6},{5,7},{6,4},{7,5},{8,10},{9,11},{10,... | collective-permute-start | bytes 835592 | tf_op jit(solution)/shard_map/ppermute | solution.py:242
  49.3 0.3 shard_map.99.refs_0_
  49.6 0.9 %collective-permute-start.18 = (f32[136,512]{1,0:T(8,128)S(1)}, f32[136,512]{1,0:T(8,128)S(1)}, u32[]{:S(2)}, u32[]{:S(2)}) collective-permute-start(f32[136,512]{1,0:T(8,128)S(1)} %shard_map.99.refs_0_), channel_id=1, source_target_pairs={{0,2},{1,3},{2,0},{3,1},{4,6},{5,7},{6,4},{7,5},{8,10},{9,11},{10,... | collective-permute-start | bytes 835592 | tf_op jit(solution)/shard_map/ppermute | solution.py:242
  50.5 6.8 %collective-permute-done.15.refs_1_ = f32[136,512]{1,0:T(8,128)S(1)} collective-permute-done((f32[136,512]{1,0:T(8,128)S(1)}, f32[136,512]{1,0:T(8,128)S(1)}, u32[]{:S(2)}, u32[]{:S(2)}) %collective-permute-start.15) | collective-permute-done | bytes 278560 | tf_op jit(solution)/shard_map/ppermute | solution.py:242
  57.3 1.0 %shard_map.96 = (f32[128,512]{1,0:T(8,128)S(1)}, f32[512,512]{1,0:T(8,128)}) custom-call(s32[1]{0:T(128)} %bitcast.rank, f32[136,512]{1,0:T(8,128)S(1)} %shard_map.95.refs_0_, f32[136,512]{1,0:T(8,128)S(1)} %collective-permute-done.15.refs_1_, f32[64,512]{1,0:T(8,128)S(1)} %shard_map.89.refs_4_.refs_2_, ...), custom_call_target="tpu_custom_call" | custom-call | tf_op jit(solution)/shard_map/pallas_call | solution.py:325
  58.4 0.1 collective-permute-start.16
  58.5 3.9 %collective-permute-done.18.refs_1_ = f32[136,512]{1,0:T(8,128)S(1)} collective-permute-done((f32[136,512]{1,0:T(8,128)S(1)}, f32[136,512]{1,0:T(8,128)S(1)}, u32[]{:S(2)}, u32[]{:S(2)}) %collective-permute-start.18) | collective-permute-done | bytes 278560 | tf_op jit(solution)/shard_map/ppermute | solution.py:242
  62.4 0.3 shard_map.100.refs_2_
  62.6 0.1 collective-permute-start.19
  62.7 0.6 shard_map.97
  63.4 0.9 %collective-permute-done.19.refs_3_ = f32[128,512]{1,0:T(8,128)S(1)} collective-permute-done((f32[128,512]{1,0:T(8,128)S(1)}, f32[128,512]{1,0:T(8,128)S(1)}, u32[]{:S(2)}, u32[]{:S(2)}) %collective-permute-start.19) | collective-permute-done | bytes 262176 | tf_op jit(solution)/shard_map/ppermute | solution.py:242
  64.2 1.4 %shard_map.101 = f32[512,512]{1,0:T(8,128)} custom-call(s32[1]{0:T(128)} %bitcast.2.half, f32[512,512]{1,0:T(8,128)S(1)} %copy-done, f32[128,512]{1,0:T(8,128)S(1)} %get-tuple-element.56.refs_0_, f32[128,512]{1,0:T(8,128)S(1)} %get-tuple-element.57.refs_1_, f32[128,512]{1,0:T(8,128)S(1)} %shard_map.100.refs_2_, f32[128,512]{1,0:T(8,128)S(1)} %collective-permute-done.19.refs_3_), custom_call_target="tpu_custom_call" | custom-call | tf_op jit(solution)/shard_map/pallas_call | solution.py:337
  (16 shorter events, 0.0 us)
Async XLA Ops:
  4.0 9.3 %collective-permute-start = (f32[72,512]{1,0:T(8,128)S(1)}, f32[72,512]{1,0:T(8,128)S(1)}, u32[]{:S(2)}, u32[]{:S(2)}) collective-permute-start(f32[72,512]{1,0:T(8,128)S(1)} %get-tuple-element.38), channel_id=1, source_target_pairs={{0,12},{4,8},{8,4},{12,0},{16,28},{20,24},{24,20},{28,16},{1,13},{... | collective-permute-start | bytes 442376 | tf_op jit(solution)/shard_map/ppermute | solution.py:242
  8.1 8.3 %collective-permute-start.1 = (f32[72,512]{1,0:T(8,128)S(1)}, f32[72,512]{1,0:T(8,128)S(1)}, u32[]{:S(2)}, u32[]{:S(2)}) collective-permute-start(f32[72,512]{1,0:T(8,128)S(1)} %get-tuple-element.39), channel_id=1, source_target_pairs={{0,8},{4,12},{8,0},{12,4},{16,24},{20,28},{24,16},{28,20},{1,9},{5... | collective-permute-start | bytes 442376 | tf_op jit(solution)/shard_map/ppermute | solution.py:242
  8.5 9.8 %collective-permute-start.2 = (f32[72,512]{1,0:T(8,128)S(1)}, f32[72,512]{1,0:T(8,128)S(1)}, u32[]{:S(2)}, u32[]{:S(2)}) collective-permute-start(f32[72,512]{1,0:T(8,128)S(1)} %get-tuple-element.40), channel_id=1, source_target_pairs={{0,4},{4,0},{8,12},{12,8},{16,20},{20,16},{24,28},{28,24},{1,5},{5... | collective-permute-start | bytes 442376 | tf_op jit(solution)/shard_map/ppermute | solution.py:242
  9.9 12.5 %collective-permute-start.7 = (f32[72,512]{1,0:T(8,128)S(1)}, f32[72,512]{1,0:T(8,128)S(1)}, u32[]{:S(2)}, u32[]{:S(2)}) collective-permute-start(f32[72,512]{1,0:T(8,128)S(1)} %get-tuple-element.49), channel_id=1, source_target_pairs={{0,12},{4,8},{8,4},{12,0},{16,28},{20,24},{24,20},{28,16},{1,13},{... | collective-permute-start | bytes 442376 | tf_op jit(solution)/shard_map/ppermute | solution.py:242
  12.8 9.6 %collective-permute-start.8 = (f32[72,512]{1,0:T(8,128)S(1)}, f32[72,512]{1,0:T(8,128)S(1)}, u32[]{:S(2)}, u32[]{:S(2)}) collective-permute-start(f32[72,512]{1,0:T(8,128)S(1)} %get-tuple-element.50), channel_id=1, source_target_pairs={{0,8},{4,12},{8,0},{12,4},{16,24},{20,28},{24,16},{28,20},{1,9},{5... | collective-permute-start | bytes 442376 | tf_op jit(solution)/shard_map/ppermute | solution.py:242
  13.3 9.1 %collective-permute-start.9 = (f32[72,512]{1,0:T(8,128)S(1)}, f32[72,512]{1,0:T(8,128)S(1)}, u32[]{:S(2)}, u32[]{:S(2)}) collective-permute-start(f32[72,512]{1,0:T(8,128)S(1)} %get-tuple-element.51), channel_id=1, source_target_pairs={{0,4},{4,0},{8,12},{12,8},{16,20},{20,16},{24,28},{28,24},{1,5},{5... | collective-permute-start | bytes 442376 | tf_op jit(solution)/shard_map/ppermute | solution.py:242
  18.7 9.1 %collective-permute-start.3 = (f32[72,512]{1,0:T(8,128)S(1)}, f32[72,512]{1,0:T(8,128)S(1)}, u32[]{:S(2)}, u32[]{:S(2)}) collective-permute-start(f32[72,512]{1,0:T(8,128)S(1)} %shard_map.88.refs_0_), channel_id=1, source_target_pairs={{0,24},{4,28},{8,16},{12,20},{16,8},{20,12},{24,0},{28,4},{1,25},{... | collective-permute-start | bytes 442376 | tf_op jit(solution)/shard_map/ppermute | solution.py:242
  22.4 15.4 %copy-start.2 = (f32[512,512]{1,0:T(8,128)S(1)}, f32[512,512]{1,0:T(8,128)}, u32[]{:S(2)}) copy-start(f32[512,512]{1,0:T(8,128)} %w_key.1) | copy-start | bytes 3145732
  22.8 15.0 %copy-start.1 = (f32[512,512]{1,0:T(8,128)S(1)}, f32[512,512]{1,0:T(8,128)}, u32[]{:S(2)}) copy-start(f32[512,512]{1,0:T(8,128)} %queries.1) | copy-start | bytes 3145732
  22.8 11.2 %collective-permute-start.10 = (f32[72,512]{1,0:T(8,128)S(1)}, f32[72,512]{1,0:T(8,128)S(1)}, u32[]{:S(2)}, u32[]{:S(2)}) collective-permute-start(f32[72,512]{1,0:T(8,128)S(1)} %shard_map.92.refs_0_), channel_id=1, source_target_pairs={{0,24},{4,28},{8,16},{12,20},{16,8},{20,12},{24,0},{28,4},{1,25},{... | collective-permute-start | bytes 442376 | tf_op jit(solution)/shard_map/ppermute | solution.py:242
  28.0 8.6 %collective-permute-start.4 = (f32[64,512]{1,0:T(8,128)S(1)}, f32[64,512]{1,0:T(8,128)S(1)}, u32[]{:S(2)}, u32[]{:S(2)}) collective-permute-start(f32[64,512]{1,0:T(8,128)S(1)} %shard_map.89.refs_4_.refs_2_), channel_id=1, source_target_pairs={{0,4},{4,0},{8,12},{12,8},{16,20},{20,16},{24,28},{28,24},{1,5},{5... | collective-permute-start | bytes 393224 | tf_op jit(solution)/shard_map/ppermute | solution.py:242
  28.1 10.7 %collective-permute-start.5 = (f32[64,512]{1,0:T(8,128)S(1)}, f32[64,512]{1,0:T(8,128)S(1)}, u32[]{:S(2)}, u32[]{:S(2)}) collective-permute-start(f32[64,512]{1,0:T(8,128)S(1)} %shard_map.89.refs_4_.refs_2_), channel_id=1, source_target_pairs={{0,8},{4,12},{8,0},{12,4},{16,24},{20,28},{24,16},{28,20},{1,9},{5... | collective-permute-start | bytes 393224 | tf_op jit(solution)/shard_map/ppermute | solution.py:242
  32.8 7.8 %collective-permute-start.6 = (f32[64,512]{1,0:T(8,128)S(1)}, f32[64,512]{1,0:T(8,128)S(1)}, u32[]{:S(2)}, u32[]{:S(2)}) collective-permute-start(f32[64,512]{1,0:T(8,128)S(1)} %shard_map.89.refs_4_.refs_2_), channel_id=1, source_target_pairs={{0,12},{4,8},{8,4},{12,0},{16,28},{20,24},{24,20},{28,16},{1,13},{... | collective-permute-start | bytes 393224 | tf_op jit(solution)/shard_map/ppermute | solution.py:242
  34.2 9.2 %collective-permute-start.11 = (f32[64,512]{1,0:T(8,128)S(1)}, f32[64,512]{1,0:T(8,128)S(1)}, u32[]{:S(2)}, u32[]{:S(2)}) collective-permute-start(f32[64,512]{1,0:T(8,128)S(1)} %shard_map.93.refs_0_.refs_6_), channel_id=1, source_target_pairs={{0,4},{4,0},{8,12},{12,8},{16,20},{20,16},{24,28},{28,24},{1,5},{5... | collective-permute-start | bytes 393224 | tf_op jit(solution)/shard_map/ppermute | solution.py:242
  34.9 8.5 %collective-permute-start.12 = (f32[64,512]{1,0:T(8,128)S(1)}, f32[64,512]{1,0:T(8,128)S(1)}, u32[]{:S(2)}, u32[]{:S(2)}) collective-permute-start(f32[64,512]{1,0:T(8,128)S(1)} %shard_map.93.refs_0_.refs_6_), channel_id=1, source_target_pairs={{0,8},{4,12},{8,0},{12,4},{16,24},{20,28},{24,16},{28,20},{1,9},{5... | collective-permute-start | bytes 393224 | tf_op jit(solution)/shard_map/ppermute | solution.py:242
  36.6 7.4 %collective-permute-start.13 = (f32[64,512]{1,0:T(8,128)S(1)}, f32[64,512]{1,0:T(8,128)S(1)}, u32[]{:S(2)}, u32[]{:S(2)}) collective-permute-start(f32[64,512]{1,0:T(8,128)S(1)} %shard_map.93.refs_0_.refs_6_), channel_id=1, source_target_pairs={{0,12},{4,8},{8,4},{12,0},{16,28},{20,24},{24,20},{28,16},{1,13},{... | collective-permute-start | bytes 393224 | tf_op jit(solution)/shard_map/ppermute | solution.py:242
  40.5 0.7 %copy-start.3 = (f32[512]{0:T(512)S(1)}, f32[512]{0:T(512)}, u32[]{:S(2)}) copy-start(f32[512]{0:T(512)} %param.10) | copy-start | bytes 6148
  45.4 2.1 %collective-permute-start.14 = (f32[136,512]{1,0:T(8,128)S(1)}, f32[136,512]{1,0:T(8,128)S(1)}, u32[]{:S(2)}, u32[]{:S(2)}) collective-permute-start(f32[136,512]{1,0:T(8,128)S(1)} %get-tuple-element.53), channel_id=1, source_target_pairs={{0,1},{1,0},{2,3},{3,2},{4,5},{5,4},{6,7},{7,6},{8,9},{9,8},{10,11... | collective-permute-start | bytes 835592 | tf_op jit(solution)/shard_map/ppermute | solution.py:242
  46.9 2.4 %collective-permute-start.17 = (f32[136,512]{1,0:T(8,128)S(1)}, f32[136,512]{1,0:T(8,128)S(1)}, u32[]{:S(2)}, u32[]{:S(2)}) collective-permute-start(f32[136,512]{1,0:T(8,128)S(1)} %get-tuple-element.61), channel_id=1, source_target_pairs={{0,1},{1,0},{2,3},{3,2},{4,5},{5,4},{6,7},{7,6},{8,9},{9,8},{10,11... | collective-permute-start | bytes 835592 | tf_op jit(solution)/shard_map/ppermute | solution.py:242
  47.8 9.6 %collective-permute-start.15 = (f32[136,512]{1,0:T(8,128)S(1)}, f32[136,512]{1,0:T(8,128)S(1)}, u32[]{:S(2)}, u32[]{:S(2)}) collective-permute-start(f32[136,512]{1,0:T(8,128)S(1)} %shard_map.95.refs_0_), channel_id=1, source_target_pairs={{0,2},{1,3},{2,0},{3,1},{4,6},{5,7},{6,4},{7,5},{8,10},{9,11},{10,... | collective-permute-start | bytes 835592 | tf_op jit(solution)/shard_map/ppermute | solution.py:242
  49.6 13.1 %copy-start = (f32[512,512]{1,0:T(8,128)S(1)}, f32[512,512]{1,0:T(8,128)}, u32[]{:S(2)}) copy-start(f32[512,512]{1,0:T(8,128)} %w_value.3) | copy-start | bytes 3145732
  49.6 12.7 %collective-permute-start.18 = (f32[136,512]{1,0:T(8,128)S(1)}, f32[136,512]{1,0:T(8,128)S(1)}, u32[]{:S(2)}, u32[]{:S(2)}) collective-permute-start(f32[136,512]{1,0:T(8,128)S(1)} %shard_map.99.refs_0_), channel_id=1, source_target_pairs={{0,2},{1,3},{2,0},{3,1},{4,6},{5,7},{6,4},{7,5},{8,10},{9,11},{10,... | collective-permute-start | bytes 835592 | tf_op jit(solution)/shard_map/ppermute | solution.py:242
  58.4 4.4 %collective-permute-start.16 = (f32[128,512]{1,0:T(8,128)S(1)}, f32[128,512]{1,0:T(8,128)S(1)}, u32[]{:S(2)}, u32[]{:S(2)}) collective-permute-start(f32[128,512]{1,0:T(8,128)S(1)} %get-tuple-element.55.refs_0_), channel_id=1, source_target_pairs={{0,1},{1,0},{2,3},{3,2},{4,5},{5,4},{6,7},{7,6},{8,9},{9,8},{10,11... | collective-permute-start | bytes 786440 | tf_op jit(solution)/shard_map/ppermute | solution.py:242
  62.6 1.6 %collective-permute-start.19 = (f32[128,512]{1,0:T(8,128)S(1)}, f32[128,512]{1,0:T(8,128)S(1)}, u32[]{:S(2)}, u32[]{:S(2)}) collective-permute-start(f32[128,512]{1,0:T(8,128)S(1)} %shard_map.100.refs_2_), channel_id=1, source_target_pairs={{0,1},{1,0},{2,3},{3,2},{4,5},{5,4},{6,7},{7,6},{8,9},{9,8},{10,11... | collective-permute-start | bytes 786440 | tf_op jit(solution)/shard_map/ppermute | solution.py:242

commit v3 on v2

--- a/solution.py
+++ b/solution.py
@@ -11,7 +11,7 @@
 STAT = 8
 CHUNKS = 2
 F32, BF16 = jnp.float32, jnp.bfloat16
-PARAMS = pltpu.CompilerParams(vmem_limit_bytes=24 * 1024 * 1024)
+PARAMS = pltpu.CompilerParams(vmem_limit_bytes=16 * 1024 * 1024)
 VMEM = pl.BlockSpec(memory_space=pltpu.VMEM)
 SMEM = pl.BlockSpec(memory_space=pltpu.SMEM)
 ANY = pl.BlockSpec(memory_space=pltpu.HBM)
@@ -148,17 +148,23 @@
     refs[-1][...] = latents[:rows] + weighted / total
 
 
-def query_kernel(half, queries, w_key, *outs, halves, scale):
-    weight = split(w_key[...])
+def query_kernel(half, queries, w_key, gain, *rest, halves, scale):
+    outs, (buf, wbuf, sems) = rest[:2 * CHUNKS + 1], rest[2 * CHUNKS + 1:]
     rows = queries.shape[0] // halves // CHUNKS
-    for b in range(CHUNKS):
-        picked = []
+    copies = [pltpu.make_async_copy(w_key, wbuf, sems.at[CHUNKS, 0]), pltpu.make_async_copy(gain, outs[-1], sems.at[CHUNKS, 1])]
+    for b in range(CHUNKS):
         for k in range(halves):
             at = pl.multiple_of((half[0] ^ k) * (rows * CHUNKS) + b * rows, 8)
-            picked.append(queries[pl.ds(at, rows), :])
-        hi, lo = split(dot3(split(jnp.concatenate(picked, axis=0) * scale), weight, NT))
-        outs[2 * b][...] = hi
-        outs[2 * b + 1][...] = lo
+            copies.append(pltpu.make_async_copy(
+                queries.at[pl.ds(at, rows), :], buf.at[pl.ds((b * halves + k) * rows, rows), :], sems.at[b, k]))
+    for copy in copies:
+        copy.start()
+    for copy in copies:
+        copy.wait()
+    weight = split(wbuf[...])
+    for b in range(CHUNKS):
+        at = pl.ds(b * halves * rows, halves * rows)
+        outs[2 * b][...], outs[2 * b + 1][...] = split(dot3(split(buf[at, :] * scale), weight, NT))
 
 
 def normed_of(states, gain):
@@ -240,6 +246,10 @@
 
 def swap(value, axis, n, mask):
     return lax.ppermute(value, axis, [(i, i ^ mask) for i in range(n)])
+
+
+def in_hbm(*arrays):
+    return [pltpu.with_memory_space_constraint(x, pltpu.HBM) for x in arrays]
 
 
 def shards(latents, pixel_keys, pixel_values, norm_gain, w_key, w_value, pixel_queries, *, npix, nlat):
@@ -273,7 +283,7 @@
         [packed] * group + [chunk] * CHUNKS + [(keys_shape, BF16)] * 4,
         [SMEM, ANY, ANY, ANY],
         [pltpu.VMEM(keys_shape, F32), pltpu.VMEM(keys_shape, F32), pltpu.SemaphoreType.DMA((CHUNKS, group)),
-         pltpu.SemaphoreType.DMA((4,)), pltpu.SemaphoreType.DMA((4,))])(rank, *[pltpu.with_memory_space_constraint(x, pltpu.HBM) for x in (latents, pixel_keys, pixel_values)])
+         pltpu.SemaphoreType.DMA((4,)), pltpu.SemaphoreType.DMA((4,))])(rank, *in_hbm(latents, pixel_keys, pixel_values))
     latent_chunks = first[group:group + CHUNKS]
     operands = first[group + CHUNKS:]
     partials = [first[:group]]
@@ -281,12 +291,14 @@
         partials.append(call(
             functools.partial(partial_kernel, scale=scale), [packed] * group, [VMEM] * 5, ())(latent_chunks[a], *operands))
 
-    pieces = [[part[0]] + [swap(part[k], "pix", npix, k) for k in range(group - 1, 0, -1)]
+    pieces = [[part[0]] + [swap(part[k], "pix", npix, k) for k in range(1, group)]
               for part in partials]
     queries = call(
         functools.partial(query_kernel, halves=halves, scale=scale),
-        [((pixel_queries.shape[0] // CHUNKS, depth), BF16)] * (2 * CHUNKS),
-        [SMEM, VMEM, VMEM], ())(half, pixel_queries, w_key)
+        [((pixel_queries.shape[0] // CHUNKS, depth), BF16)] * (2 * CHUNKS) + [(1, depth)],
+        [SMEM, ANY, ANY, ANY],
+        [pltpu.VMEM(pixel_queries.shape, F32), pltpu.VMEM(w_key.shape, F32), pltpu.SemaphoreType.DMA((CHUNKS + 1, 2))])(half, *in_hbm(pixel_queries, w_key, norm_gain.reshape(1, depth)))
+    gain, queries = queries[-1], queries[:-1]
 
     for mask in outer:
         for a in range(CHUNKS):
@@ -299,7 +311,6 @@
             functools.partial(state_kernel, rows=rows), [(rows, depth)], [VMEM] * (1 + len(pieces[a])), ())(latent_chunks[a], *pieces[a])
         states.append([state] + [swap(state, "pix", npix, k) for k in range(1, group)])
 
-    gain = norm_gain.reshape(1, depth)
     qchunk = pixel_queries.shape[0] // CHUNKS
     qrows = qchunk // halves
     early = call(

time: 65.8 us -> 64.5 us (0.980)
  starting transfers between devices: 30.2 us -> 27.4 us
  Pallas kernels: 15.7 us -> 17.3 us
  waiting for transfers between devices: 18.1 us -> 18.8 us
  local copies, waits for them, and re-layouts: 0.7 us -> 0.01 us
    ppermute x20, starting transfers between devices: 30.2 us -> 27.4 us  [swap(): return lax.ppermute(value, axis, [(i, i ^ mask) for i in range(n)])]
    pallas_call x1, Pallas kernels: 1.05 us -> 2.59 us  [window(): call(functools.partial(query_kernel, halves=halves, scale=scale), [((pixe...]
    ppermute x20, waiting for transfers between devices: 18.1 us -> 18.8 us  [swap(): return lax.ppermute(value, axis, [(i, i ^ mask) for i in range(n)])]
    unnamed x8 -> x2, local copies, waits for them, and re-layouts: 0.7 us -> 0.01 us
  transfers between devices with their start and end apart: 20 -> 20, of which waited for: 8 -> 9; matrix products, arithmetic and copies ran while one was open for 0% -> 0% of each run, Pallas kernels for 15% -> 17%
where the time goes in v3:
time: 64.5 us; the launch traced here: 64.3 us
  starting transfers between devices  27.4 us (42%)
  waiting for transfers between devices  18.8 us (29%)
  Pallas kernels  17.3 us (27%)
  between operations  0.8 us (1%)
    ppermute x20, starting transfers between devices, swap(): return lax.ppermute(value, axis, [(i, i ^ mask) for i in range(n)])  27.4 us
    ppermute x20, waiting for transfers between devices, swap(): return lax.ppermute(value, axis, [(i, i ^ mask) for i in range(n)])  18.8 us
    pallas_call x1, Pallas kernels, window(): call(functools.partial(first_kernel, blocks=group, scale=scale), [packed]...  3.37 us
    pallas_call x2, Pallas kernels, window(): call(functools.partial(late_kernel, blocks=group, halves=halves), [packed...  2.82 us
    pallas_call x1, Pallas kernels, window(): call(functools.partial(query_kernel, halves=halves, scale=scale), [((pixe...  2.59 us
    pallas_call x1, Pallas kernels, window(): call(functools.partial(early_kernel, blocks=group), [(qchunk, depth), (qc...  2.18 us
    pallas_call x1, Pallas kernels, window(): call(functools.partial(out_kernel, halves=halves), [pixel_queries.shape],...  1.37 us
  transfers between devices with their start and end apart: 20, of which 9 were waited for; matrix products, arithmetic and copies ran while one was open for 0% of the time, Pallas kernels for 17%

profile of v3, /device:TPU:0, one launch (start us, length us, event | category | flops | bytes accessed | tf_op | source)
XLA Modules:
  0.0 64.3 jit_solution(13625913749512498965)
XLA Ops:
  0.6 3.4 %shard_map.87 = (f32[72,512]{1,0:T(8,128)S(1)}, f32[72,512]{1,0:T(8,128)S(1)}, f32[72,512]{1,0:T(8,128)S(1)}, f32[72,512]{1,0:T(8,128)S(1)}, f32[256,512]{1,0:T(...) custom-call(s32[1]{0:T(128)} %bitcast.rank, ...), custom_call_target="tpu_custom_call" | custom-call | tf_op jit(solution)/shard_map/pallas_call | solution.py:281
  4.0 3.1 %collective-permute-start = (f32[72,512]{1,0:T(8,128)S(1)}, f32[72,512]{1,0:T(8,128)S(1)}, u32[]{:S(2)}, u32[]{:S(2)}) collective-permute-start(f32[72,512]{1,0:T(8,128)S(1)} %get-tuple-element.40), channel_id=1, source_target_pairs={{0,4},{4,0},{8,12},{12,8},{16,20},{20,16},{24,28},{28,24},{1,5},{5... | collective-permute-start | bytes 442376 | tf_op jit(solution)/shard_map/ppermute | solution.py:248
  7.1 1.6 %collective-permute-start.1 = (f32[72,512]{1,0:T(8,128)S(1)}, f32[72,512]{1,0:T(8,128)S(1)}, u32[]{:S(2)}, u32[]{:S(2)}) collective-permute-start(f32[72,512]{1,0:T(8,128)S(1)} %get-tuple-element.41), channel_id=1, source_target_pairs={{0,8},{4,12},{8,0},{12,4},{16,24},{20,28},{24,16},{28,20},{1,9},{5... | collective-permute-start | bytes 442376 | tf_op jit(solution)/shard_map/ppermute | solution.py:248
  8.7 0.0 collective-permute-start.2
  8.7 1.2 %shard_map.91 = (f32[72,512]{1,0:T(8,128)S(1)}, f32[72,512]{1,0:T(8,128)S(1)}, f32[72,512]{1,0:T(8,128)S(1)}, f32[72,512]{1,0:T(8,128)S(1)}) custom-call(f32[256,512]{1,0:T(8,128)S(1)} %get-tuple-element.45.queries.latents, bf16[512,512]{1,0:T(8,128)(2,1)S(1)} %get-tuple-element.46.kh, bf16[512,512]{1,0:T(8,128)(2,1)S(1)} %get-tuple-element.47.kl, ...), custom_call_target="tpu_custom_call" | custom-call | tf_op jit(solution)/shard_map/pallas_call | solution.py:291
  9.9 2.0 %collective-permute-start.7 = (f32[72,512]{1,0:T(8,128)S(1)}, f32[72,512]{1,0:T(8,128)S(1)}, u32[]{:S(2)}, u32[]{:S(2)}) collective-permute-start(f32[72,512]{1,0:T(8,128)S(1)} %get-tuple-element.51), channel_id=1, source_target_pairs={{0,4},{4,0},{8,12},{12,8},{16,20},{20,16},{24,28},{28,24},{1,5},{5... | collective-permute-start | bytes 442376 | tf_op jit(solution)/shard_map/ppermute | solution.py:248
  11.8 1.6 %collective-permute-start.8 = (f32[72,512]{1,0:T(8,128)S(1)}, f32[72,512]{1,0:T(8,128)S(1)}, u32[]{:S(2)}, u32[]{:S(2)}) collective-permute-start(f32[72,512]{1,0:T(8,128)S(1)} %get-tuple-element.52), channel_id=1, source_target_pairs={{0,8},{4,12},{8,0},{12,4},{16,24},{20,28},{24,16},{28,20},{1,9},{5... | collective-permute-start | bytes 442376 | tf_op jit(solution)/shard_map/ppermute | solution.py:248
  13.4 0.5 collective-permute-start.9
  13.9 0.0 collective-permute-done.1.refs_2_
  13.9 2.4 %collective-permute-done.2.refs_3_ = f32[72,512]{1,0:T(8,128)S(1)} collective-permute-done((f32[72,512]{1,0:T(8,128)S(1)}, f32[72,512]{1,0:T(8,128)S(1)}, u32[]{:S(2)}, u32[]{:S(2)}) %collective-permute-start.2) | collective-permute-done | bytes 147488 | tf_op jit(solution)/shard_map/ppermute | solution.py:248
  16.3 0.4 shard_map.88.refs_0_
  16.7 4.2 %collective-permute-start.3 = (f32[72,512]{1,0:T(8,128)S(1)}, f32[72,512]{1,0:T(8,128)S(1)}, u32[]{:S(2)}, u32[]{:S(2)}) collective-permute-start(f32[72,512]{1,0:T(8,128)S(1)} %shard_map.88.refs_0_), channel_id=1, source_target_pairs={{0,24},{4,28},{8,16},{12,20},{16,8},{20,12},{24,0},{28,4},{1,25},{... | collective-permute-start | bytes 442376 | tf_op jit(solution)/shard_map/ppermute | solution.py:248
  20.9 1.5 %collective-permute-done.9.refs_3_ = f32[72,512]{1,0:T(8,128)S(1)} collective-permute-done((f32[72,512]{1,0:T(8,128)S(1)}, f32[72,512]{1,0:T(8,128)S(1)}, u32[]{:S(2)}, u32[]{:S(2)}) %collective-permute-start.9) | collective-permute-done | bytes 147488 | tf_op jit(solution)/shard_map/ppermute | solution.py:248
  22.4 0.4 shard_map.92.refs_0_
  22.7 4.6 %collective-permute-start.10 = (f32[72,512]{1,0:T(8,128)S(1)}, f32[72,512]{1,0:T(8,128)S(1)}, u32[]{:S(2)}, u32[]{:S(2)}) collective-permute-start(f32[72,512]{1,0:T(8,128)S(1)} %shard_map.92.refs_0_), channel_id=1, source_target_pairs={{0,24},{4,28},{8,16},{12,20},{16,8},{20,12},{24,0},{28,4},{1,25},{... | collective-permute-start | bytes 442376 | tf_op jit(solution)/shard_map/ppermute | solution.py:248
  27.4 1.2 %collective-permute-done.3.refs_1_ = f32[72,512]{1,0:T(8,128)S(1)} collective-permute-done((f32[72,512]{1,0:T(8,128)S(1)}, f32[72,512]{1,0:T(8,128)S(1)}, u32[]{:S(2)}, u32[]{:S(2)}) %collective-permute-start.3) | collective-permute-done | bytes 147488 | tf_op jit(solution)/shard_map/ppermute | solution.py:248
  28.5 0.2 shard_map.89.refs_4_.refs_2_
  28.8 2.0 %collective-permute-start.4 = (f32[64,512]{1,0:T(8,128)S(1)}, f32[64,512]{1,0:T(8,128)S(1)}, u32[]{:S(2)}, u32[]{:S(2)}) collective-permute-start(f32[64,512]{1,0:T(8,128)S(1)} %shard_map.89.refs_4_.refs_2_), channel_id=1, source_target_pairs={{0,4},{4,0},{8,12},{12,8},{16,20},{20,16},{24,28},{28,24},{1,5},{5... | collective-permute-start | bytes 393224 | tf_op jit(solution)/shard_map/ppermute | solution.py:248
  30.8 0.2 collective-permute-start.5
  31.0 1.3 %collective-permute-start.6 = (f32[64,512]{1,0:T(8,128)S(1)}, f32[64,512]{1,0:T(8,128)S(1)}, u32[]{:S(2)}, u32[]{:S(2)}) collective-permute-start(f32[64,512]{1,0:T(8,128)S(1)} %shard_map.89.refs_4_.refs_2_), channel_id=1, source_target_pairs={{0,12},{4,8},{8,4},{12,0},{16,28},{20,24},{24,20},{28,16},{1,13},{... | collective-permute-start | bytes 393224 | tf_op jit(solution)/shard_map/ppermute | solution.py:248
  32.3 0.0 collective-permute-done.10.refs_1_
  32.4 0.2 shard_map.93.refs_0_.refs_6_
  32.6 2.2 %collective-permute-start.11 = (f32[64,512]{1,0:T(8,128)S(1)}, f32[64,512]{1,0:T(8,128)S(1)}, u32[]{:S(2)}, u32[]{:S(2)}) collective-permute-start(f32[64,512]{1,0:T(8,128)S(1)} %shard_map.93.refs_0_.refs_6_), channel_id=1, source_target_pairs={{0,4},{4,0},{8,12},{12,8},{16,20},{20,16},{24,28},{28,24},{1,5},{5... | collective-permute-start | bytes 393224 | tf_op jit(solution)/shard_map/ppermute | solution.py:248
  34.8 0.0 collective-permute-start.12
  34.8 0.7 %collective-permute-done.4.refs_5_.refs_3_ = f32[64,512]{1,0:T(8,128)S(1)} collective-permute-done((f32[64,512]{1,0:T(8,128)S(1)}, f32[64,512]{1,0:T(8,128)S(1)}, u32[]{:S(2)}, u32[]{:S(2)}) %collective-permute-start.4) | collective-permute-done | bytes 131104 | tf_op jit(solution)/shard_map/ppermute | solution.py:248
  35.5 0.8 %collective-permute-start.13 = (f32[64,512]{1,0:T(8,128)S(1)}, f32[64,512]{1,0:T(8,128)S(1)}, u32[]{:S(2)}, u32[]{:S(2)}) collective-permute-start(f32[64,512]{1,0:T(8,128)S(1)} %shard_map.93.refs_0_.refs_6_), channel_id=1, source_target_pairs={{0,12},{4,8},{8,4},{12,0},{16,28},{20,24},{24,20},{28,16},{1,13},{... | collective-permute-start | bytes 393224 | tf_op jit(solution)/shard_map/ppermute | solution.py:248
  36.4 2.6 %shard_map.86 = (bf16[256,512]{1,0:T(8,128)(2,1)S(1)}, bf16[256,512]{1,0:T(8,128)(2,1)S(1)}, bf16[256,512]{1,0:T(8,128)(2,1)S(1)}, bf16[256,512]{1,0:T(8,128)(2,1)S(1)}, f32[1,512]{1,0:T(1,128)S(1)}) custom-call(s32[1]{0:T(128)} %bitcast.1.half, f32[512,512]{1,0:T(8,128)} %queries.1, f32[512,512]{1,0:T(8,128)} %w_key.1, f32[1,512]{1,0:T(1,128)} %bitcast.3), custom_call_target="tpu_custom_call" | custom-call | tf_op jit(solution)/shard_map/pallas_call | solution.py:296
  39.0 0.0 collective-permute-done.5.refs_6_.refs_4_
  39.0 2.2 %shard_map.90 = (f32[256,512]{1,0:T(8,128)S(1)}, f32[256,128]{1,0:T(8,128)S(1)}, f32[256,512]{1,0:T(8,128)S(1)}, f32[256,128]{1,0:T(8,128)S(1)}) custom-call(f32[1,512]{1,0:T(1,128)S(1)} %get-tuple-element.33.gain, bf16[256,512]{1,0:T(8,128)(2,1)S(1)} %get-tuple-element.34.refs_0_.qh, bf16[256,512]{1,0:T(8,128)(2,1)S(1)} %get-tuple-element.35.refs_1_.ql, ...), custom_call_target="tpu_custom_call" | custom-call | tf_op jit(solution)/shard_map/pallas_call | solution.py:316
  41.2 0.3 collective-permute-done.12.refs_2_.refs_8_
  41.4 1.2 %collective-permute-done.13.refs_3_.refs_9_ = f32[64,512]{1,0:T(8,128)S(1)} collective-permute-done((f32[64,512]{1,0:T(8,128)S(1)}, f32[64,512]{1,0:T(8,128)S(1)}, u32[]{:S(2)}, u32[]{:S(2)}) %collective-permute-start.13) | collective-permute-done | bytes 131104 | tf_op jit(solution)/shard_map/ppermute | solution.py:248
  42.7 1.4 %shard_map.94 = (f32[136,512]{1,0:T(8,128)S(1)}, f32[136,512]{1,0:T(8,128)S(1)}) custom-call(f32[1,512]{1,0:T(1,128)S(1)} %get-tuple-element.33.gain, bf16[256,512]{1,0:T(8,128)(2,1)S(1)} %get-tuple-element.34.refs_0_.qh, bf16[256,512]{1,0:T(8,128)(2,1)S(1)} %get-tuple-element.35.refs_1_.ql, f32[256,512]{1,0:T(8,128)S(1)} %get-tuple-element.43.acc, ...), custom_call_target="tpu_custom_call" | custom-call | tf_op jit(solution)/shard_map/pallas_call | solution.py:322
  44.1 0.1 collective-permute-start.14
  44.2 1.4 %shard_map.98 = (f32[136,512]{1,0:T(8,128)S(1)}, f32[136,512]{1,0:T(8,128)S(1)}) custom-call(f32[1,512]{1,0:T(1,128)S(1)} %get-tuple-element.33.gain, bf16[256,512]{1,0:T(8,128)(2,1)S(1)} %get-tuple-element.36.refs_2_.qh, bf16[256,512]{1,0:T(8,128)(2,1)S(1)} %get-tuple-element.37.refs_3_.ql, f32[256,512]{1,0:T(8,128)S(1)} %get-tuple-element.60.acc, ...), custom_call_target="tpu_custom_call" | custom-call | tf_op jit(solution)/shard_map/pallas_call | solution.py:322
  45.6 0.6 collective-permute-start.17
  46.1 0.3 shard_map.95.refs_0_
  46.4 1.5 %collective-permute-start.15 = (f32[136,512]{1,0:T(8,128)S(1)}, f32[136,512]{1,0:T(8,128)S(1)}, u32[]{:S(2)}, u32[]{:S(2)}) collective-permute-start(f32[136,512]{1,0:T(8,128)S(1)} %shard_map.95.refs_0_), channel_id=1, source_target_pairs={{0,2},{1,3},{2,0},{3,1},{4,6},{5,7},{6,4},{7,5},{8,10},{9,11},{10,... | collective-permute-start | bytes 835592 | tf_op jit(solution)/shard_map/ppermute | solution.py:248
  48.0 0.3 shard_map.99.refs_0_
  48.3 0.9 %collective-permute-start.18 = (f32[136,512]{1,0:T(8,128)S(1)}, f32[136,512]{1,0:T(8,128)S(1)}, u32[]{:S(2)}, u32[]{:S(2)}) collective-permute-start(f32[136,512]{1,0:T(8,128)S(1)} %shard_map.99.refs_0_), channel_id=1, source_target_pairs={{0,2},{1,3},{2,0},{3,1},{4,6},{5,7},{6,4},{7,5},{8,10},{9,11},{10,... | collective-permute-start | bytes 835592 | tf_op jit(solution)/shard_map/ppermute | solution.py:248
  49.2 6.8 %collective-permute-done.15.refs_1_ = f32[136,512]{1,0:T(8,128)S(1)} collective-permute-done((f32[136,512]{1,0:T(8,128)S(1)}, f32[136,512]{1,0:T(8,128)S(1)}, u32[]{:S(2)}, u32[]{:S(2)}) %collective-permute-start.15) | collective-permute-done | bytes 278560 | tf_op jit(solution)/shard_map/ppermute | solution.py:248
  56.0 1.0 %shard_map.96 = (f32[128,512]{1,0:T(8,128)S(1)}, f32[512,512]{1,0:T(8,128)}) custom-call(s32[1]{0:T(128)} %bitcast.rank, f32[136,512]{1,0:T(8,128)S(1)} %shard_map.95.refs_0_, f32[136,512]{1,0:T(8,128)S(1)} %collective-permute-done.15.refs_1_, f32[64,512]{1,0:T(8,128)S(1)} %shard_map.89.refs_4_.refs_2_, ...), custom_call_target="tpu_custom_call" | custom-call | tf_op jit(solution)/shard_map/pallas_call | solution.py:336
  57.0 0.1 collective-permute-start.16
  57.1 3.9 %collective-permute-done.18.refs_1_ = f32[136,512]{1,0:T(8,128)S(1)} collective-permute-done((f32[136,512]{1,0:T(8,128)S(1)}, f32[136,512]{1,0:T(8,128)S(1)}, u32[]{:S(2)}, u32[]{:S(2)}) %collective-permute-start.18) | collective-permute-done | bytes 278560 | tf_op jit(solution)/shard_map/ppermute | solution.py:248
  61.0 0.3 shard_map.100.refs_2_
  61.3 0.1 collective-permute-start.19
  61.4 0.6 shard_map.97
  62.0 0.9 %collective-permute-done.19.refs_3_ = f32[128,512]{1,0:T(8,128)S(1)} collective-permute-done((f32[128,512]{1,0:T(8,128)S(1)}, f32[128,512]{1,0:T(8,128)S(1)}, u32[]{:S(2)}, u32[]{:S(2)}) %collective-permute-start.19) | collective-permute-done | bytes 262176 | tf_op jit(solution)/shard_map/ppermute | solution.py:248
  62.9 1.4 %shard_map.101 = f32[512,512]{1,0:T(8,128)} custom-call(s32[1]{0:T(128)} %bitcast.1.half, f32[512,512]{1,0:T(8,128)S(1)} %copy-done, f32[128,512]{1,0:T(8,128)S(1)} %get-tuple-element.58.refs_0_, f32[128,512]{1,0:T(8,128)S(1)} %get-tuple-element.59.refs_1_, f32[128,512]{1,0:T(8,128)S(1)} %shard_map.100.refs_2_, f32[128,512]{1,0:T(8,128)S(1)} %collective-permute-done.19.refs_3_), custom_call_target="tpu_custom_call" | custom-call | tf_op jit(solution)/shard_map/pallas_call | solution.py:348
  (10 shorter events, 0.0 us)
Async XLA Ops:
  4.0 9.4 %collective-permute-start = (f32[72,512]{1,0:T(8,128)S(1)}, f32[72,512]{1,0:T(8,128)S(1)}, u32[]{:S(2)}, u32[]{:S(2)}) collective-permute-start(f32[72,512]{1,0:T(8,128)S(1)} %get-tuple-element.40), channel_id=1, source_target_pairs={{0,4},{4,0},{8,12},{12,8},{16,20},{20,16},{24,28},{28,24},{1,5},{5... | collective-permute-start | bytes 442376 | tf_op jit(solution)/shard_map/ppermute | solution.py:248
  7.1 6.8 %collective-permute-start.1 = (f32[72,512]{1,0:T(8,128)S(1)}, f32[72,512]{1,0:T(8,128)S(1)}, u32[]{:S(2)}, u32[]{:S(2)}) collective-permute-start(f32[72,512]{1,0:T(8,128)S(1)} %get-tuple-element.41), channel_id=1, source_target_pairs={{0,8},{4,12},{8,0},{12,4},{16,24},{20,28},{24,16},{28,20},{1,9},{5... | collective-permute-start | bytes 442376 | tf_op jit(solution)/shard_map/ppermute | solution.py:248
  8.7 7.7 %collective-permute-start.2 = (f32[72,512]{1,0:T(8,128)S(1)}, f32[72,512]{1,0:T(8,128)S(1)}, u32[]{:S(2)}, u32[]{:S(2)}) collective-permute-start(f32[72,512]{1,0:T(8,128)S(1)} %get-tuple-element.42), channel_id=1, source_target_pairs={{0,12},{4,8},{8,4},{12,0},{16,28},{20,24},{24,20},{28,16},{1,13},{... | collective-permute-start | bytes 442376 | tf_op jit(solution)/shard_map/ppermute | solution.py:248
  9.9 11.1 %collective-permute-start.7 = (f32[72,512]{1,0:T(8,128)S(1)}, f32[72,512]{1,0:T(8,128)S(1)}, u32[]{:S(2)}, u32[]{:S(2)}) collective-permute-start(f32[72,512]{1,0:T(8,128)S(1)} %get-tuple-element.51), channel_id=1, source_target_pairs={{0,4},{4,0},{8,12},{12,8},{16,20},{20,16},{24,28},{28,24},{1,5},{5... | collective-permute-start | bytes 442376 | tf_op jit(solution)/shard_map/ppermute | solution.py:248
  11.8 9.1 %collective-permute-start.8 = (f32[72,512]{1,0:T(8,128)S(1)}, f32[72,512]{1,0:T(8,128)S(1)}, u32[]{:S(2)}, u32[]{:S(2)}) collective-permute-start(f32[72,512]{1,0:T(8,128)S(1)} %get-tuple-element.52), channel_id=1, source_target_pairs={{0,8},{4,12},{8,0},{12,4},{16,24},{20,28},{24,16},{28,20},{1,9},{5... | collective-permute-start | bytes 442376 | tf_op jit(solution)/shard_map/ppermute | solution.py:248
  13.4 9.0 %collective-permute-start.9 = (f32[72,512]{1,0:T(8,128)S(1)}, f32[72,512]{1,0:T(8,128)S(1)}, u32[]{:S(2)}, u32[]{:S(2)}) collective-permute-start(f32[72,512]{1,0:T(8,128)S(1)} %get-tuple-element.53), channel_id=1, source_target_pairs={{0,12},{4,8},{8,4},{12,0},{16,28},{20,24},{24,20},{28,16},{1,13},{... | collective-permute-start | bytes 442376 | tf_op jit(solution)/shard_map/ppermute | solution.py:248
  16.7 11.9 %collective-permute-start.3 = (f32[72,512]{1,0:T(8,128)S(1)}, f32[72,512]{1,0:T(8,128)S(1)}, u32[]{:S(2)}, u32[]{:S(2)}) collective-permute-start(f32[72,512]{1,0:T(8,128)S(1)} %shard_map.88.refs_0_), channel_id=1, source_target_pairs={{0,24},{4,28},{8,16},{12,20},{16,8},{20,12},{24,0},{28,4},{1,25},{... | collective-permute-start | bytes 442376 | tf_op jit(solution)/shard_map/ppermute | solution.py:248
  22.7 9.6 %collective-permute-start.10 = (f32[72,512]{1,0:T(8,128)S(1)}, f32[72,512]{1,0:T(8,128)S(1)}, u32[]{:S(2)}, u32[]{:S(2)}) collective-permute-start(f32[72,512]{1,0:T(8,128)S(1)} %shard_map.92.refs_0_), channel_id=1, source_target_pairs={{0,24},{4,28},{8,16},{12,20},{16,8},{20,12},{24,0},{28,4},{1,25},{... | collective-permute-start | bytes 442376 | tf_op jit(solution)/shard_map/ppermute | solution.py:248
  28.8 6.8 %collective-permute-start.4 = (f32[64,512]{1,0:T(8,128)S(1)}, f32[64,512]{1,0:T(8,128)S(1)}, u32[]{:S(2)}, u32[]{:S(2)}) collective-permute-start(f32[64,512]{1,0:T(8,128)S(1)} %shard_map.89.refs_4_.refs_2_), channel_id=1, source_target_pairs={{0,4},{4,0},{8,12},{12,8},{16,20},{20,16},{24,28},{28,24},{1,5},{5... | collective-permute-start | bytes 393224 | tf_op jit(solution)/shard_map/ppermute | solution.py:248
  30.8 8.2 %collective-permute-start.5 = (f32[64,512]{1,0:T(8,128)S(1)}, f32[64,512]{1,0:T(8,128)S(1)}, u32[]{:S(2)}, u32[]{:S(2)}) collective-permute-start(f32[64,512]{1,0:T(8,128)S(1)} %shard_map.89.refs_4_.refs_2_), channel_id=1, source_target_pairs={{0,8},{4,12},{8,0},{12,4},{16,24},{20,28},{24,16},{28,20},{1,9},{5... | collective-permute-start | bytes 393224 | tf_op jit(solution)/shard_map/ppermute | solution.py:248
  31.0 7.9 %collective-permute-start.6 = (f32[64,512]{1,0:T(8,128)S(1)}, f32[64,512]{1,0:T(8,128)S(1)}, u32[]{:S(2)}, u32[]{:S(2)}) collective-permute-start(f32[64,512]{1,0:T(8,128)S(1)} %shard_map.89.refs_4_.refs_2_), channel_id=1, source_target_pairs={{0,12},{4,8},{8,4},{12,0},{16,28},{20,24},{24,20},{28,16},{1,13},{... | collective-permute-start | bytes 393224 | tf_op jit(solution)/shard_map/ppermute | solution.py:248
  32.6 8.6 %collective-permute-start.11 = (f32[64,512]{1,0:T(8,128)S(1)}, f32[64,512]{1,0:T(8,128)S(1)}, u32[]{:S(2)}, u32[]{:S(2)}) collective-permute-start(f32[64,512]{1,0:T(8,128)S(1)} %shard_map.93.refs_0_.refs_6_), channel_id=1, source_target_pairs={{0,4},{4,0},{8,12},{12,8},{16,20},{20,16},{24,28},{28,24},{1,5},{5... | collective-permute-start | bytes 393224 | tf_op jit(solution)/shard_map/ppermute | solution.py:248
  34.8 6.6 %collective-permute-start.12 = (f32[64,512]{1,0:T(8,128)S(1)}, f32[64,512]{1,0:T(8,128)S(1)}, u32[]{:S(2)}, u32[]{:S(2)}) collective-permute-start(f32[64,512]{1,0:T(8,128)S(1)} %shard_map.93.refs_0_.refs_6_), channel_id=1, source_target_pairs={{0,8},{4,12},{8,0},{12,4},{16,24},{20,28},{24,16},{28,20},{1,9},{5... | collective-permute-start | bytes 393224 | tf_op jit(solution)/shard_map/ppermute | solution.py:248
  35.5 7.1 %collective-permute-start.13 = (f32[64,512]{1,0:T(8,128)S(1)}, f32[64,512]{1,0:T(8,128)S(1)}, u32[]{:S(2)}, u32[]{:S(2)}) collective-permute-start(f32[64,512]{1,0:T(8,128)S(1)} %shard_map.93.refs_0_.refs_6_), channel_id=1, source_target_pairs={{0,12},{4,8},{8,4},{12,0},{16,28},{20,24},{24,20},{28,16},{1,13},{... | collective-permute-start | bytes 393224 | tf_op jit(solution)/shard_map/ppermute | solution.py:248
  44.1 2.1 %collective-permute-start.14 = (f32[136,512]{1,0:T(8,128)S(1)}, f32[136,512]{1,0:T(8,128)S(1)}, u32[]{:S(2)}, u32[]{:S(2)}) collective-permute-start(f32[136,512]{1,0:T(8,128)S(1)} %get-tuple-element.55), channel_id=1, source_target_pairs={{0,1},{1,0},{2,3},{3,2},{4,5},{5,4},{6,7},{7,6},{8,9},{9,8},{10,11... | collective-permute-start | bytes 835592 | tf_op jit(solution)/shard_map/ppermute | solution.py:248
  45.6 2.4 %collective-permute-start.17 = (f32[136,512]{1,0:T(8,128)S(1)}, f32[136,512]{1,0:T(8,128)S(1)}, u32[]{:S(2)}, u32[]{:S(2)}) collective-permute-start(f32[136,512]{1,0:T(8,128)S(1)} %get-tuple-element.63), channel_id=1, source_target_pairs={{0,1},{1,0},{2,3},{3,2},{4,5},{5,4},{6,7},{7,6},{8,9},{9,8},{10,11... | collective-permute-start | bytes 835592 | tf_op jit(solution)/shard_map/ppermute | solution.py:248
  46.4 9.6 %collective-permute-start.15 = (f32[136,512]{1,0:T(8,128)S(1)}, f32[136,512]{1,0:T(8,128)S(1)}, u32[]{:S(2)}, u32[]{:S(2)}) collective-permute-start(f32[136,512]{1,0:T(8,128)S(1)} %shard_map.95.refs_0_), channel_id=1, source_target_pairs={{0,2},{1,3},{2,0},{3,1},{4,6},{5,7},{6,4},{7,5},{8,10},{9,11},{10,... | collective-permute-start | bytes 835592 | tf_op jit(solution)/shard_map/ppermute | solution.py:248
  48.3 13.1 %copy-start = (f32[512,512]{1,0:T(8,128)S(1)}, f32[512,512]{1,0:T(8,128)}, u32[]{:S(2)}) copy-start(f32[512,512]{1,0:T(8,128)} %w_value.3) | copy-start | bytes 3145732
  48.3 12.7 %collective-permute-start.18 = (f32[136,512]{1,0:T(8,128)S(1)}, f32[136,512]{1,0:T(8,128)S(1)}, u32[]{:S(2)}, u32[]{:S(2)}) collective-permute-start(f32[136,512]{1,0:T(8,128)S(1)} %shard_map.99.refs_0_), channel_id=1, source_target_pairs={{0,2},{1,3},{2,0},{3,1},{4,6},{5,7},{6,4},{7,5},{8,10},{9,11},{10,... | collective-permute-start | bytes 835592 | tf_op jit(solution)/shard_map/ppermute | solution.py:248
  57.0 4.4 %collective-permute-start.16 = (f32[128,512]{1,0:T(8,128)S(1)}, f32[128,512]{1,0:T(8,128)S(1)}, u32[]{:S(2)}, u32[]{:S(2)}) collective-permute-start(f32[128,512]{1,0:T(8,128)S(1)} %get-tuple-element.57.refs_0_), channel_id=1, source_target_pairs={{0,1},{1,0},{2,3},{3,2},{4,5},{5,4},{6,7},{7,6},{8,9},{9,8},{10,11... | collective-permute-start | bytes 786440 | tf_op jit(solution)/shard_map/ppermute | solution.py:248
  61.3 1.6 %collective-permute-start.19 = (f32[128,512]{1,0:T(8,128)S(1)}, f32[128,512]{1,0:T(8,128)S(1)}, u32[]{:S(2)}, u32[]{:S(2)}) collective-permute-start(f32[128,512]{1,0:T(8,128)S(1)} %shard_map.100.refs_2_), channel_id=1, source_target_pairs={{0,1},{1,0},{2,3},{3,2},{4,5},{5,4},{6,7},{7,6},{8,9},{9,8},{10,11... | collective-permute-start | bytes 786440 | tf_op jit(solution)/shard_map/ppermute | solution.py:248

commit v4 on v3

--- a/solution.py
+++ b/solution.py
@@ -217,28 +217,35 @@
 
 
 def project_kernel(w_value, *refs):
-    weight = split(w_value[...])
+    *refs, hi_out, lo_out = refs
+    hi_out[...], lo_out[...] = split(w_value[...])
     half = len(refs) // 2
     for src, dst in zip(refs[:half], refs[half:]):
-        dst[...] = dot3(split(src[...]), weight, NN)
-
-
-def out_kernel(half, w_value, *refs, halves):
-    ready, last = refs[:halves * (CHUNKS - 1)], refs[halves * (CHUNKS - 1):halves * CHUNKS]
-    out, buf, sems = refs[halves * CHUNKS:]
-    rows = last[0].shape[0]
-
-    def copy_out(src, b, k):
+        dst[...] = dot3(split(src[...]), (hi_out[...], lo_out[...]), NN)
+
+
+def own_kernel(hi, lo, src, dst):
+    dst[...] = dot3(split(src[...]), (hi[...], lo[...]), NN)
+
+
+def out_kernel(half, hi, lo, *refs, halves):
+    count = halves * CHUNKS
+    ready, last = refs[:count - halves + 1], refs[count - halves + 1:count]
+    out, buf, sems = refs[count:]
+    rows = ready[0].shape[0]
+
+    def copy_out(src, i):
+        b, k = divmod(i, halves)
         at = pl.multiple_of((half[0] ^ k) * (rows * CHUNKS) + b * rows, 8)
         return pltpu.make_async_copy(src, out.at[pl.ds(at, rows), :], sems.at[b, k])
 
-    copies = [copy_out(ready[b * halves + k], b, k) for b in range(CHUNKS - 1) for k in range(halves)]
+    copies = [copy_out(src, i) for i, src in enumerate(ready)]
     for copy in copies:
         copy.start()
-    weight = split(w_value[...])
-    for k in range(halves):
-        buf[pl.ds(k * rows, rows), :] = dot3(split(last[k][...]), weight, NN)
-        copies.append(copy_out(buf.at[pl.ds(k * rows, rows), :], CHUNKS - 1, k))
+    for i, src in enumerate(last):
+        at = pl.ds(i * rows, rows)
+        buf[at, :] = dot3(split(src[...]), (hi[...], lo[...]), NN)
+        copies.append(copy_out(buf.at[at, :], len(ready) + i))
         copies[-1].start()
     for copy in copies:
         copy.wait()
@@ -343,13 +350,16 @@
         means.append([mean] + [swap(mean, "lat", nlat, k) for k in range(1, halves)])
     ready = []
     for b in range(CHUNKS - 1):
-        ready += call(
-            project_kernel, [(qrows, depth)] * halves, [VMEM] * (1 + halves), ())(w_value, *means[b])
+        *done, hi, lo = call(
+            project_kernel, [(qrows, depth)] * halves + [(w_value.shape, BF16)] * 2,
+            [VMEM] * (1 + halves), ())(w_value, *means[b])
+        ready += done
+    own, = call(own_kernel, [(qrows, depth)], [VMEM] * 3, ())(hi, lo, means[-1][0])
     pixel_out, = call(
         functools.partial(out_kernel, halves=halves), [pixel_queries.shape],
-        [SMEM, VMEM] + [VMEM] * (halves * CHUNKS),
-        [pltpu.VMEM((halves * qrows, depth), F32), pltpu.SemaphoreType.DMA((CHUNKS, halves))],
-        [ANY])(half, w_value, *ready, *means[-1])
+        [SMEM] + [VMEM] * (2 + halves * CHUNKS),
+        [pltpu.VMEM((max(halves - 1, 1) * qrows, depth), F32), pltpu.SemaphoreType.DMA((CHUNKS, halves))],
+        [ANY])(half, hi, lo, *ready, own, *means[-1][1:])
     return latent_state, pixel_out
 
 

time: 64.5 us -> 64.2 us (level)
  transfers between devices with their start and end apart: 20 -> 20, of which waited for: 9 -> 9; matrix products, arithmetic and copies ran while one was open for 0% -> 0% of each run, Pallas kernels for 17% -> 18%
where the time goes in v4:
time: 64.2 us; the launch traced here: 64 us
  starting transfers between devices  27.4 us (43%)
  waiting for transfers between devices  18.4 us (29%)
  Pallas kernels  17.5 us (27%)
  between operations  0.81 us (1%)
    ppermute x20, starting transfers between devices, swap(): return lax.ppermute(value, axis, [(i, i ^ mask) for i in range(n)])  27.4 us
    ppermute x20, waiting for transfers between devices, swap(): return lax.ppermute(value, axis, [(i, i ^ mask) for i in range(n)])  18.4 us
    pallas_call x1, Pallas kernels, window(): call(functools.partial(first_kernel, blocks=group, scale=scale), [packed]...  3.37 us
    pallas_call x2, Pallas kernels, window(): call(functools.partial(late_kernel, blocks=group, halves=halves), [packed...  2.83 us
    pallas_call x1, Pallas kernels, window(): call(functools.partial(query_kernel, halves=halves, scale=scale), [((pixe...  2.59 us
    pallas_call x1, Pallas kernels, window(): call(functools.partial(early_kernel, blocks=group), [(qchunk, depth), (qc...  2.18 us
  transfers between devices with their start and end apart: 20, of which 9 were waited for; matrix products, arithmetic and copies ran while one was open for 0% of the time, Pallas kernels for 18%

profile of v4, /device:TPU:0, one launch (start us, length us, event | category | flops | bytes accessed | tf_op | source)
XLA Modules:
  0.0 64.0 jit_solution(77110201247917334)
XLA Ops:
  0.6 3.4 %shard_map.87 = (f32[72,512]{1,0:T(8,128)S(1)}, f32[72,512]{1,0:T(8,128)S(1)}, f32[72,512]{1,0:T(8,128)S(1)}, f32[72,512]{1,0:T(8,128)S(1)}, f32[256,512]{1,0:T(...) custom-call(s32[1]{0:T(128)} %bitcast.rank, ...), custom_call_target="tpu_custom_call" | custom-call | tf_op jit(solution)/shard_map/pallas_call | solution.py:288
  4.0 3.1 %collective-permute-start = (f32[72,512]{1,0:T(8,128)S(1)}, f32[72,512]{1,0:T(8,128)S(1)}, u32[]{:S(2)}, u32[]{:S(2)}) collective-permute-start(f32[72,512]{1,0:T(8,128)S(1)} %get-tuple-element.42), channel_id=1, source_target_pairs={{0,4},{4,0},{8,12},{12,8},{16,20},{20,16},{24,28},{28,24},{1,5},{5... | collective-permute-start | bytes 442376 | tf_op jit(solution)/shard_map/ppermute | solution.py:255
  7.1 1.6 %collective-permute-start.1 = (f32[72,512]{1,0:T(8,128)S(1)}, f32[72,512]{1,0:T(8,128)S(1)}, u32[]{:S(2)}, u32[]{:S(2)}) collective-permute-start(f32[72,512]{1,0:T(8,128)S(1)} %get-tuple-element.43), channel_id=1, source_target_pairs={{0,8},{4,12},{8,0},{12,4},{16,24},{20,28},{24,16},{28,20},{1,9},{5... | collective-permute-start | bytes 442376 | tf_op jit(solution)/shard_map/ppermute | solution.py:255
  8.7 0.0 collective-permute-start.2
  8.7 1.2 %shard_map.91 = (f32[72,512]{1,0:T(8,128)S(1)}, f32[72,512]{1,0:T(8,128)S(1)}, f32[72,512]{1,0:T(8,128)S(1)}, f32[72,512]{1,0:T(8,128)S(1)}) custom-call(f32[256,512]{1,0:T(8,128)S(1)} %get-tuple-element.47.queries.latents, bf16[512,512]{1,0:T(8,128)(2,1)S(1)} %get-tuple-element.48.kh, bf16[512,512]{1,0:T(8,128)(2,1)S(1)} %get-tuple-element.49.kl, ...), custom_call_target="tpu_custom_call" | custom-call | tf_op jit(solution)/shard_map/pallas_call | solution.py:298
  9.9 2.0 %collective-permute-start.7 = (f32[72,512]{1,0:T(8,128)S(1)}, f32[72,512]{1,0:T(8,128)S(1)}, u32[]{:S(2)}, u32[]{:S(2)}) collective-permute-start(f32[72,512]{1,0:T(8,128)S(1)} %get-tuple-element.53), channel_id=1, source_target_pairs={{0,4},{4,0},{8,12},{12,8},{16,20},{20,16},{24,28},{28,24},{1,5},{5... | collective-permute-start | bytes 442376 | tf_op jit(solution)/shard_map/ppermute | solution.py:255
  11.8 1.6 %collective-permute-start.8 = (f32[72,512]{1,0:T(8,128)S(1)}, f32[72,512]{1,0:T(8,128)S(1)}, u32[]{:S(2)}, u32[]{:S(2)}) collective-permute-start(f32[72,512]{1,0:T(8,128)S(1)} %get-tuple-element.54), channel_id=1, source_target_pairs={{0,8},{4,12},{8,0},{12,4},{16,24},{20,28},{24,16},{28,20},{1,9},{5... | collective-permute-start | bytes 442376 | tf_op jit(solution)/shard_map/ppermute | solution.py:255
  13.4 0.5 collective-permute-start.9
  13.9 0.0 collective-permute-done.1.refs_2_
  13.9 2.4 %collective-permute-done.2.refs_3_ = f32[72,512]{1,0:T(8,128)S(1)} collective-permute-done((f32[72,512]{1,0:T(8,128)S(1)}, f32[72,512]{1,0:T(8,128)S(1)}, u32[]{:S(2)}, u32[]{:S(2)}) %collective-permute-start.2) | collective-permute-done | bytes 147488 | tf_op jit(solution)/shard_map/ppermute | solution.py:255
  16.3 0.4 shard_map.88.refs_0_
  16.7 4.2 %collective-permute-start.3 = (f32[72,512]{1,0:T(8,128)S(1)}, f32[72,512]{1,0:T(8,128)S(1)}, u32[]{:S(2)}, u32[]{:S(2)}) collective-permute-start(f32[72,512]{1,0:T(8,128)S(1)} %shard_map.88.refs_0_), channel_id=1, source_target_pairs={{0,24},{4,28},{8,16},{12,20},{16,8},{20,12},{24,0},{28,4},{1,25},{... | collective-permute-start | bytes 442376 | tf_op jit(solution)/shard_map/ppermute | solution.py:255
  20.9 1.5 %collective-permute-done.9.refs_3_ = f32[72,512]{1,0:T(8,128)S(1)} collective-permute-done((f32[72,512]{1,0:T(8,128)S(1)}, f32[72,512]{1,0:T(8,128)S(1)}, u32[]{:S(2)}, u32[]{:S(2)}) %collective-permute-start.9) | collective-permute-done | bytes 147488 | tf_op jit(solution)/shard_map/ppermute | solution.py:255
  22.4 0.4 shard_map.92.refs_0_
  22.7 4.6 %collective-permute-start.10 = (f32[72,512]{1,0:T(8,128)S(1)}, f32[72,512]{1,0:T(8,128)S(1)}, u32[]{:S(2)}, u32[]{:S(2)}) collective-permute-start(f32[72,512]{1,0:T(8,128)S(1)} %shard_map.92.refs_0_), channel_id=1, source_target_pairs={{0,24},{4,28},{8,16},{12,20},{16,8},{20,12},{24,0},{28,4},{1,25},{... | collective-permute-start | bytes 442376 | tf_op jit(solution)/shard_map/ppermute | solution.py:255
  27.4 1.2 %collective-permute-done.3.refs_1_ = f32[72,512]{1,0:T(8,128)S(1)} collective-permute-done((f32[72,512]{1,0:T(8,128)S(1)}, f32[72,512]{1,0:T(8,128)S(1)}, u32[]{:S(2)}, u32[]{:S(2)}) %collective-permute-start.3) | collective-permute-done | bytes 147488 | tf_op jit(solution)/shard_map/ppermute | solution.py:255
  28.5 0.2 shard_map.89.refs_4_.refs_2_
  28.8 2.0 %collective-permute-start.4 = (f32[64,512]{1,0:T(8,128)S(1)}, f32[64,512]{1,0:T(8,128)S(1)}, u32[]{:S(2)}, u32[]{:S(2)}) collective-permute-start(f32[64,512]{1,0:T(8,128)S(1)} %shard_map.89.refs_4_.refs_2_), channel_id=1, source_target_pairs={{0,4},{4,0},{8,12},{12,8},{16,20},{20,16},{24,28},{28,24},{1,5},{5... | collective-permute-start | bytes 393224 | tf_op jit(solution)/shard_map/ppermute | solution.py:255
  30.8 0.2 collective-permute-start.5
  31.0 1.3 %collective-permute-start.6 = (f32[64,512]{1,0:T(8,128)S(1)}, f32[64,512]{1,0:T(8,128)S(1)}, u32[]{:S(2)}, u32[]{:S(2)}) collective-permute-start(f32[64,512]{1,0:T(8,128)S(1)} %shard_map.89.refs_4_.refs_2_), channel_id=1, source_target_pairs={{0,12},{4,8},{8,4},{12,0},{16,28},{20,24},{24,20},{28,16},{1,13},{... | collective-permute-start | bytes 393224 | tf_op jit(solution)/shard_map/ppermute | solution.py:255
  32.3 0.0 collective-permute-done.10.refs_1_
  32.4 0.2 shard_map.93.refs_0_.refs_6_
  32.6 2.2 %collective-permute-start.11 = (f32[64,512]{1,0:T(8,128)S(1)}, f32[64,512]{1,0:T(8,128)S(1)}, u32[]{:S(2)}, u32[]{:S(2)}) collective-permute-start(f32[64,512]{1,0:T(8,128)S(1)} %shard_map.93.refs_0_.refs_6_), channel_id=1, source_target_pairs={{0,4},{4,0},{8,12},{12,8},{16,20},{20,16},{24,28},{28,24},{1,5},{5... | collective-permute-start | bytes 393224 | tf_op jit(solution)/shard_map/ppermute | solution.py:255
  34.8 0.0 collective-permute-start.12
  34.8 0.7 %collective-permute-done.4.refs_5_.refs_3_ = f32[64,512]{1,0:T(8,128)S(1)} collective-permute-done((f32[64,512]{1,0:T(8,128)S(1)}, f32[64,512]{1,0:T(8,128)S(1)}, u32[]{:S(2)}, u32[]{:S(2)}) %collective-permute-start.4) | collective-permute-done | bytes 131104 | tf_op jit(solution)/shard_map/ppermute | solution.py:255
  35.5 0.8 %collective-permute-start.13 = (f32[64,512]{1,0:T(8,128)S(1)}, f32[64,512]{1,0:T(8,128)S(1)}, u32[]{:S(2)}, u32[]{:S(2)}) collective-permute-start(f32[64,512]{1,0:T(8,128)S(1)} %shard_map.93.refs_0_.refs_6_), channel_id=1, source_target_pairs={{0,12},{4,8},{8,4},{12,0},{16,28},{20,24},{24,20},{28,16},{1,13},{... | collective-permute-start | bytes 393224 | tf_op jit(solution)/shard_map/ppermute | solution.py:255
  36.4 2.6 %shard_map.86 = (bf16[256,512]{1,0:T(8,128)(2,1)S(1)}, bf16[256,512]{1,0:T(8,128)(2,1)S(1)}, bf16[256,512]{1,0:T(8,128)(2,1)S(1)}, bf16[256,512]{1,0:T(8,128)(2,1)S(1)}, f32[1,512]{1,0:T(1,128)S(1)}) custom-call(s32[1]{0:T(128)} %bitcast.1.half, f32[512,512]{1,0:T(8,128)} %queries.1, f32[512,512]{1,0:T(8,128)} %w_key.1, f32[1,512]{1,0:T(1,128)} %bitcast.3), custom_call_target="tpu_custom_call" | custom-call | tf_op jit(solution)/shard_map/pallas_call | solution.py:303
  39.0 2.2 %shard_map.90 = (f32[256,512]{1,0:T(8,128)S(1)}, f32[256,128]{1,0:T(8,128)S(1)}, f32[256,512]{1,0:T(8,128)S(1)}, f32[256,128]{1,0:T(8,128)S(1)}) custom-call(f32[1,512]{1,0:T(1,128)S(1)} %get-tuple-element.35.gain, bf16[256,512]{1,0:T(8,128)(2,1)S(1)} %get-tuple-element.36.refs_0_.qh, bf16[256,512]{1,0:T(8,128)(2,1)S(1)} %get-tuple-element.37.refs_1_.ql, ...), custom_call_target="tpu_custom_call" | custom-call | tf_op jit(solution)/shard_map/pallas_call | solution.py:323
  41.2 0.3 collective-permute-done.12.refs_2_.refs_8_
  41.4 1.2 %collective-permute-done.13.refs_3_.refs_9_ = f32[64,512]{1,0:T(8,128)S(1)} collective-permute-done((f32[64,512]{1,0:T(8,128)S(1)}, f32[64,512]{1,0:T(8,128)S(1)}, u32[]{:S(2)}, u32[]{:S(2)}) %collective-permute-start.13) | collective-permute-done | bytes 131104 | tf_op jit(solution)/shard_map/ppermute | solution.py:255
  42.7 1.4 %shard_map.94 = (f32[136,512]{1,0:T(8,128)S(1)}, f32[136,512]{1,0:T(8,128)S(1)}) custom-call(f32[1,512]{1,0:T(1,128)S(1)} %get-tuple-element.35.gain, bf16[256,512]{1,0:T(8,128)(2,1)S(1)} %get-tuple-element.36.refs_0_.qh, bf16[256,512]{1,0:T(8,128)(2,1)S(1)} %get-tuple-element.37.refs_1_.ql, f32[256,512]{1,0:T(8,128)S(1)} %get-tuple-element.45.acc, ...), custom_call_target="tpu_custom_call" | custom-call | tf_op jit(solution)/shard_map/pallas_call | solution.py:329
  44.1 0.1 collective-permute-start.14
  44.2 1.4 %shard_map.98 = (f32[136,512]{1,0:T(8,128)S(1)}, f32[136,512]{1,0:T(8,128)S(1)}) custom-call(f32[1,512]{1,0:T(1,128)S(1)} %get-tuple-element.35.gain, bf16[256,512]{1,0:T(8,128)(2,1)S(1)} %get-tuple-element.38.refs_2_.qh, bf16[256,512]{1,0:T(8,128)(2,1)S(1)} %get-tuple-element.39.refs_3_.ql, f32[256,512]{1,0:T(8,128)S(1)} %get-tuple-element.64.acc, ...), custom_call_target="tpu_custom_call" | custom-call | tf_op jit(solution)/shard_map/pallas_call | solution.py:329
  45.6 0.6 collective-permute-start.17
  46.1 0.3 shard_map.95.refs_0_
  46.5 1.5 %collective-permute-start.15 = (f32[136,512]{1,0:T(8,128)S(1)}, f32[136,512]{1,0:T(8,128)S(1)}, u32[]{:S(2)}, u32[]{:S(2)}) collective-permute-start(f32[136,512]{1,0:T(8,128)S(1)} %shard_map.95.refs_0_), channel_id=1, source_target_pairs={{0,2},{1,3},{2,0},{3,1},{4,6},{5,7},{6,4},{7,5},{8,10},{9,11},{10,... | collective-permute-start | bytes 835592 | tf_op jit(solution)/shard_map/ppermute | solution.py:255
  48.0 0.3 shard_map.99.refs_0_
  48.3 0.9 %collective-permute-start.18 = (f32[136,512]{1,0:T(8,128)S(1)}, f32[136,512]{1,0:T(8,128)S(1)}, u32[]{:S(2)}, u32[]{:S(2)}) collective-permute-start(f32[136,512]{1,0:T(8,128)S(1)} %shard_map.99.refs_0_), channel_id=1, source_target_pairs={{0,2},{1,3},{2,0},{3,1},{4,6},{5,7},{6,4},{7,5},{8,10},{9,11},{10,... | collective-permute-start | bytes 835592 | tf_op jit(solution)/shard_map/ppermute | solution.py:255
  49.2 6.8 %collective-permute-done.15.refs_1_ = f32[136,512]{1,0:T(8,128)S(1)} collective-permute-done((f32[136,512]{1,0:T(8,128)S(1)}, f32[136,512]{1,0:T(8,128)S(1)}, u32[]{:S(2)}, u32[]{:S(2)}) %collective-permute-start.15) | collective-permute-done | bytes 278560 | tf_op jit(solution)/shard_map/ppermute | solution.py:255
  56.0 1.0 %shard_map.96 = (f32[128,512]{1,0:T(8,128)S(1)}, f32[512,512]{1,0:T(8,128)}) custom-call(s32[1]{0:T(128)} %bitcast.rank, f32[136,512]{1,0:T(8,128)S(1)} %shard_map.95.refs_0_, f32[136,512]{1,0:T(8,128)S(1)} %collective-permute-done.15.refs_1_, f32[64,512]{1,0:T(8,128)S(1)} %shard_map.89.refs_4_.refs_2_, ...), custom_call_target="tpu_custom_call" | custom-call | tf_op jit(solution)/shard_map/pallas_call | solution.py:343
  57.0 0.1 collective-permute-start.16
  57.1 3.9 %collective-permute-done.18.refs_1_ = f32[136,512]{1,0:T(8,128)S(1)} collective-permute-done((f32[136,512]{1,0:T(8,128)S(1)}, f32[136,512]{1,0:T(8,128)S(1)}, u32[]{:S(2)}, u32[]{:S(2)}) %collective-permute-start.18) | collective-permute-done | bytes 278560 | tf_op jit(solution)/shard_map/ppermute | solution.py:255
  61.0 0.3 shard_map.100.src
  61.3 0.1 collective-permute-start.19
  61.4 0.7 %shard_map.97 = (f32[128,512]{1,0:T(8,128)S(1)}, f32[128,512]{1,0:T(8,128)S(1)}, bf16[512,512]{1,0:T(8,128)(2,1)S(1)}, bf16[512,512]{1,0:T(8,128)(2,1)S(1)}) custom-call(f32[512,512]{1,0:T(8,128)S(1)} %copy-done, f32[128,512]{1,0:T(8,128)S(1)} %get-tuple-element.59.refs_0_, f32[128,512]{1,0:T(8,128)S(1)} %collective-permute-done.16.refs_1_), custom_call_target="tpu_custom_call" | custom-call | tf_op jit(solution)/shard_map/pallas_call | solution.py:353
  62.1 0.4 shard_map.101.refs_2_
  62.5 0.4 collective-permute-done.19.refs_3_
  62.9 1.1 %shard_map.102 = f32[512,512]{1,0:T(8,128)} custom-call(s32[1]{0:T(128)} %bitcast.1.half, bf16[512,512]{1,0:T(8,128)(2,1)S(1)} %get-tuple-element.60.hi, bf16[512,512]{1,0:T(8,128)(2,1)S(1)} %get-tuple-element.61.lo, f32[128,512]{1,0:T(8,128)S(1)} %get-tuple-element.62.refs_0_, f32[128,512]{1,0:T(8,128)S(1)} %get-tuple-element.63.refs_1_, ...), custom_call_target="tpu_custom_call" | custom-call | tf_op jit(solution)/shard_map/pallas_call | solution.py:358
  (11 shorter events, 0.0 us)
Async XLA Ops:
  4.0 9.4 %collective-permute-start = (f32[72,512]{1,0:T(8,128)S(1)}, f32[72,512]{1,0:T(8,128)S(1)}, u32[]{:S(2)}, u32[]{:S(2)}) collective-permute-start(f32[72,512]{1,0:T(8,128)S(1)} %get-tuple-element.42), channel_id=1, source_target_pairs={{0,4},{4,0},{8,12},{12,8},{16,20},{20,16},{24,28},{28,24},{1,5},{5... | collective-permute-start | bytes 442376 | tf_op jit(solution)/shard_map/ppermute | solution.py:255
  7.1 6.8 %collective-permute-start.1 = (f32[72,512]{1,0:T(8,128)S(1)}, f32[72,512]{1,0:T(8,128)S(1)}, u32[]{:S(2)}, u32[]{:S(2)}) collective-permute-start(f32[72,512]{1,0:T(8,128)S(1)} %get-tuple-element.43), channel_id=1, source_target_pairs={{0,8},{4,12},{8,0},{12,4},{16,24},{20,28},{24,16},{28,20},{1,9},{5... | collective-permute-start | bytes 442376 | tf_op jit(solution)/shard_map/ppermute | solution.py:255
  8.7 7.7 %collective-permute-start.2 = (f32[72,512]{1,0:T(8,128)S(1)}, f32[72,512]{1,0:T(8,128)S(1)}, u32[]{:S(2)}, u32[]{:S(2)}) collective-permute-start(f32[72,512]{1,0:T(8,128)S(1)} %get-tuple-element.44), channel_id=1, source_target_pairs={{0,12},{4,8},{8,4},{12,0},{16,28},{20,24},{24,20},{28,16},{1,13},{... | collective-permute-start | bytes 442376 | tf_op jit(solution)/shard_map/ppermute | solution.py:255
  9.9 11.1 %collective-permute-start.7 = (f32[72,512]{1,0:T(8,128)S(1)}, f32[72,512]{1,0:T(8,128)S(1)}, u32[]{:S(2)}, u32[]{:S(2)}) collective-permute-start(f32[72,512]{1,0:T(8,128)S(1)} %get-tuple-element.53), channel_id=1, source_target_pairs={{0,4},{4,0},{8,12},{12,8},{16,20},{20,16},{24,28},{28,24},{1,5},{5... | collective-permute-start | bytes 442376 | tf_op jit(solution)/shard_map/ppermute | solution.py:255
  11.8 9.1 %collective-permute-start.8 = (f32[72,512]{1,0:T(8,128)S(1)}, f32[72,512]{1,0:T(8,128)S(1)}, u32[]{:S(2)}, u32[]{:S(2)}) collective-permute-start(f32[72,512]{1,0:T(8,128)S(1)} %get-tuple-element.54), channel_id=1, source_target_pairs={{0,8},{4,12},{8,0},{12,4},{16,24},{20,28},{24,16},{28,20},{1,9},{5... | collective-permute-start | bytes 442376 | tf_op jit(solution)/shard_map/ppermute | solution.py:255
  13.4 9.0 %collective-permute-start.9 = (f32[72,512]{1,0:T(8,128)S(1)}, f32[72,512]{1,0:T(8,128)S(1)}, u32[]{:S(2)}, u32[]{:S(2)}) collective-permute-start(f32[72,512]{1,0:T(8,128)S(1)} %get-tuple-element.55), channel_id=1, source_target_pairs={{0,12},{4,8},{8,4},{12,0},{16,28},{20,24},{24,20},{28,16},{1,13},{... | collective-permute-start | bytes 442376 | tf_op jit(solution)/shard_map/ppermute | solution.py:255
  16.7 11.9 %collective-permute-start.3 = (f32[72,512]{1,0:T(8,128)S(1)}, f32[72,512]{1,0:T(8,128)S(1)}, u32[]{:S(2)}, u32[]{:S(2)}) collective-permute-start(f32[72,512]{1,0:T(8,128)S(1)} %shard_map.88.refs_0_), channel_id=1, source_target_pairs={{0,24},{4,28},{8,16},{12,20},{16,8},{20,12},{24,0},{28,4},{1,25},{... | collective-permute-start | bytes 442376 | tf_op jit(solution)/shard_map/ppermute | solution.py:255
  22.7 9.6 %collective-permute-start.10 = (f32[72,512]{1,0:T(8,128)S(1)}, f32[72,512]{1,0:T(8,128)S(1)}, u32[]{:S(2)}, u32[]{:S(2)}) collective-permute-start(f32[72,512]{1,0:T(8,128)S(1)} %shard_map.92.refs_0_), channel_id=1, source_target_pairs={{0,24},{4,28},{8,16},{12,20},{16,8},{20,12},{24,0},{28,4},{1,25},{... | collective-permute-start | bytes 442376 | tf_op jit(solution)/shard_map/ppermute | solution.py:255
  28.8 6.8 %collective-permute-start.4 = (f32[64,512]{1,0:T(8,128)S(1)}, f32[64,512]{1,0:T(8,128)S(1)}, u32[]{:S(2)}, u32[]{:S(2)}) collective-permute-start(f32[64,512]{1,0:T(8,128)S(1)} %shard_map.89.refs_4_.refs_2_), channel_id=1, source_target_pairs={{0,4},{4,0},{8,12},{12,8},{16,20},{20,16},{24,28},{28,24},{1,5},{5... | collective-permute-start | bytes 393224 | tf_op jit(solution)/shard_map/ppermute | solution.py:255
  30.8 8.2 %collective-permute-start.5 = (f32[64,512]{1,0:T(8,128)S(1)}, f32[64,512]{1,0:T(8,128)S(1)}, u32[]{:S(2)}, u32[]{:S(2)}) collective-permute-start(f32[64,512]{1,0:T(8,128)S(1)} %shard_map.89.refs_4_.refs_2_), channel_id=1, source_target_pairs={{0,8},{4,12},{8,0},{12,4},{16,24},{20,28},{24,16},{28,20},{1,9},{5... | collective-permute-start | bytes 393224 | tf_op jit(solution)/shard_map/ppermute | solution.py:255
  31.0 7.9 %collective-permute-start.6 = (f32[64,512]{1,0:T(8,128)S(1)}, f32[64,512]{1,0:T(8,128)S(1)}, u32[]{:S(2)}, u32[]{:S(2)}) collective-permute-start(f32[64,512]{1,0:T(8,128)S(1)} %shard_map.89.refs_4_.refs_2_), channel_id=1, source_target_pairs={{0,12},{4,8},{8,4},{12,0},{16,28},{20,24},{24,20},{28,16},{1,13},{... | collective-permute-start | bytes 393224 | tf_op jit(solution)/shard_map/ppermute | solution.py:255
  32.6 8.6 %collective-permute-start.11 = (f32[64,512]{1,0:T(8,128)S(1)}, f32[64,512]{1,0:T(8,128)S(1)}, u32[]{:S(2)}, u32[]{:S(2)}) collective-permute-start(f32[64,512]{1,0:T(8,128)S(1)} %shard_map.93.refs_0_.refs_6_), channel_id=1, source_target_pairs={{0,4},{4,0},{8,12},{12,8},{16,20},{20,16},{24,28},{28,24},{1,5},{5... | collective-permute-start | bytes 393224 | tf_op jit(solution)/shard_map/ppermute | solution.py:255
  34.8 6.6 %collective-permute-start.12 = (f32[64,512]{1,0:T(8,128)S(1)}, f32[64,512]{1,0:T(8,128)S(1)}, u32[]{:S(2)}, u32[]{:S(2)}) collective-permute-start(f32[64,512]{1,0:T(8,128)S(1)} %shard_map.93.refs_0_.refs_6_), channel_id=1, source_target_pairs={{0,8},{4,12},{8,0},{12,4},{16,24},{20,28},{24,16},{28,20},{1,9},{5... | collective-permute-start | bytes 393224 | tf_op jit(solution)/shard_map/ppermute | solution.py:255
  35.5 7.1 %collective-permute-start.13 = (f32[64,512]{1,0:T(8,128)S(1)}, f32[64,512]{1,0:T(8,128)S(1)}, u32[]{:S(2)}, u32[]{:S(2)}) collective-permute-start(f32[64,512]{1,0:T(8,128)S(1)} %shard_map.93.refs_0_.refs_6_), channel_id=1, source_target_pairs={{0,12},{4,8},{8,4},{12,0},{16,28},{20,24},{24,20},{28,16},{1,13},{... | collective-permute-start | bytes 393224 | tf_op jit(solution)/shard_map/ppermute | solution.py:255
  44.1 2.1 %collective-permute-start.14 = (f32[136,512]{1,0:T(8,128)S(1)}, f32[136,512]{1,0:T(8,128)S(1)}, u32[]{:S(2)}, u32[]{:S(2)}) collective-permute-start(f32[136,512]{1,0:T(8,128)S(1)} %get-tuple-element.57), channel_id=1, source_target_pairs={{0,1},{1,0},{2,3},{3,2},{4,5},{5,4},{6,7},{7,6},{8,9},{9,8},{10,11... | collective-permute-start | bytes 835592 | tf_op jit(solution)/shard_map/ppermute | solution.py:255
  45.6 2.4 %collective-permute-start.17 = (f32[136,512]{1,0:T(8,128)S(1)}, f32[136,512]{1,0:T(8,128)S(1)}, u32[]{:S(2)}, u32[]{:S(2)}) collective-permute-start(f32[136,512]{1,0:T(8,128)S(1)} %get-tuple-element.67), channel_id=1, source_target_pairs={{0,1},{1,0},{2,3},{3,2},{4,5},{5,4},{6,7},{7,6},{8,9},{9,8},{10,11... | collective-permute-start | bytes 835592 | tf_op jit(solution)/shard_map/ppermute | solution.py:255
  46.5 9.6 %collective-permute-start.15 = (f32[136,512]{1,0:T(8,128)S(1)}, f32[136,512]{1,0:T(8,128)S(1)}, u32[]{:S(2)}, u32[]{:S(2)}) collective-permute-start(f32[136,512]{1,0:T(8,128)S(1)} %shard_map.95.refs_0_), channel_id=1, source_target_pairs={{0,2},{1,3},{2,0},{3,1},{4,6},{5,7},{6,4},{7,5},{8,10},{9,11},{10,... | collective-permute-start | bytes 835592 | tf_op jit(solution)/shard_map/ppermute | solution.py:255
  48.3 13.1 %copy-start = (f32[512,512]{1,0:T(8,128)S(1)}, f32[512,512]{1,0:T(8,128)}, u32[]{:S(2)}) copy-start(f32[512,512]{1,0:T(8,128)} %w_value.1) | copy-start | bytes 3145732
  48.3 12.7 %collective-permute-start.18 = (f32[136,512]{1,0:T(8,128)S(1)}, f32[136,512]{1,0:T(8,128)S(1)}, u32[]{:S(2)}, u32[]{:S(2)}) collective-permute-start(f32[136,512]{1,0:T(8,128)S(1)} %shard_map.99.refs_0_), channel_id=1, source_target_pairs={{0,2},{1,3},{2,0},{3,1},{4,6},{5,7},{6,4},{7,5},{8,10},{9,11},{10,... | collective-permute-start | bytes 835592 | tf_op jit(solution)/shard_map/ppermute | solution.py:255
  57.0 4.4 %collective-permute-start.16 = (f32[128,512]{1,0:T(8,128)S(1)}, f32[128,512]{1,0:T(8,128)S(1)}, u32[]{:S(2)}, u32[]{:S(2)}) collective-permute-start(f32[128,512]{1,0:T(8,128)S(1)} %get-tuple-element.59.refs_0_), channel_id=1, source_target_pairs={{0,1},{1,0},{2,3},{3,2},{4,5},{5,4},{6,7},{7,6},{8,9},{9,8},{10,11... | collective-permute-start | bytes 786440 | tf_op jit(solution)/shard_map/ppermute | solution.py:255
  61.3 1.6 %collective-permute-start.19 = (f32[128,512]{1,0:T(8,128)S(1)}, f32[128,512]{1,0:T(8,128)S(1)}, u32[]{:S(2)}, u32[]{:S(2)}) collective-permute-start(f32[128,512]{1,0:T(8,128)S(1)} %shard_map.100.src), channel_id=1, source_target_pairs={{0,1},{1,0},{2,3},{3,2},{4,5},{5,4},{6,7},{7,6},{8,9},{9,8},{10,11... | collective-permute-start | bytes 786440 | tf_op jit(solution)/shard_map/ppermute | solution.py:255
